TPU v7x, 32 devices: a whole 2x2x4 slice. The times are simulated.
32 devices in a mesh: rows: 16 (over z, y, x), spec: 2 (over core).
Axes of the slice: x: 2, y: 2, z: 4, core: 2. Of those that a mesh axis runs over, the one named last changes fastest.
Arguments:
- field: float32 [36, 30, 8192], P('spec', None, 'rows'), may hold values from 0.1 to 4
- group_speed: float32 [30], replicated, may hold values from 0.3 to 1
- face_angle: float32 [16384], P('rows'), may hold values from -3.140625 to 3.140625
- face_speed: float32 [16384], P('rows'), may hold values from 0.04 to 0.2
- face_cells: int32 [2, 16384], P(None, 'rows'), may hold values from 0 to 1023, as said below
- face_live: int32 [16], P('rows'), may hold values from 1 to 8, as said below
- halo_blocks: int32 [16, 2, 2], P('rows'), may hold values from 0 to 3
- cell_level: int32 [8192], P('rows'), may hold values from 0 to 2
- polar_mask: int32 [8192], P('rows'), may hold values 0 or 1
- turn_rate: float32 [8192], P('rows'), may hold values from -0.45 to 0.45
Outputs:
- advanced: float32 [36, 30, 8192], P('spec', None, 'rows')
Inputs may be any that keep to these rules, and one draw needn't show every extreme that they name: `face_cells`: row 0 is a face's lower cell, a position among its row block's own 512 cells; row 1 its upper cell, a position among the own cells followed by 2 halo blocks from the block before and 2 from the block after (128 cells each). Only the first face_live[r] of row block r's 8 face blocks carry faces; some row block has all 8 live.
All inputs are finite; a program needn't handle non-finite values. No bound on the sum of `polar_mask` on one device may be relied on, other than what follows from the above.
Results may differ from a plain program's by a relative error of at most 0.0003.
Values sent between devices are 32-bit elements; how exact they have to be, the bound alone decides.
A program may use at most 64 MiB of HBM per device.

v0:
```python
import math

import jax
import jax.numpy as jnp
from jax import lax
from jax.sharding import PartitionSpec as P

NDIR = 36
ITERS = 3


def with_halo(x, sides, width, wrap):
    for axis, dim in sides:
        size, length = (lax.axis_size(axis), x.shape[dim])
        up = [(i, (i + 1) % size) for i in range(size if wrap else size - 1)]
        down = [(j, i) for i, j in up]
        last = lax.slice_in_dim(x, length - width, length, axis=dim)
        first = lax.slice_in_dim(x, 0, width, axis=dim)
        before = lax.ppermute(last, axis, up)
        after = lax.ppermute(first, axis, down)
        x = jnp.concatenate([before, x, after], axis=dim)
    return x


def from_behind(value, axis, steps):
    count = lax.axis_size(axis)
    first, last = (max(0, -steps), min(count, count - steps))
    return lax.ppermute(value, axis, [(source, source + steps) for source in range(first, last)])


def pick_blocks(neighbour, table):
    ndir, nfreq, cdev = neighbour.shape
    view = neighbour.reshape(ndir, nfreq, cdev // 128, 128)
    return jnp.take(view, table, axis=2).reshape(ndir, nfreq, -1)


def block_flux(spectra, own_cells, own_hot, up_hot, signed_hot, forward, backward):
    low_vals = jnp.dot(
        spectra[:, :own_cells],
        own_hot,
        precision=lax.Precision.HIGHEST,
        preferred_element_type=jnp.float32,
    )
    up_vals = jnp.dot(
        spectra, up_hot, precision=lax.Precision.HIGHEST, preferred_element_type=jnp.float32
    )
    flux = forward * low_vals + backward * up_vals
    return lax.dot_general(
        flux,
        signed_hot,
        (((1,), (1,)), ((), ())),
        precision=lax.Precision.HIGHEST,
        preferred_element_type=jnp.float32,
    )


def on_device(
    field,
    group_speed,
    face_angle,
    face_speed,
    face_cells,
    face_live,
    halo_blocks,
    cell_level,
    polar_mask,
    turn_rate,
):
    dloc, nfreq, cdev = field.shape
    fdev = face_angle.shape[0]
    first_dir = lax.axis_index("spec") * dloc
    theta = ((first_dir + jnp.arange(dloc, dtype=jnp.int32)).astype(jnp.float32) + 0.5) * (
        2.0 * math.pi / NDIR
    )
    weight_turn = (polar_mask.astype(jnp.float32) * turn_rate)[None, None, :]
    area_scale = jnp.exp2(-cell_level.astype(jnp.float32))[None, None, :]
    live_count = face_live[0]
    slot_live = (jnp.arange(fdev, dtype=jnp.int32) < live_count * 128).astype(jnp.float32)
    slot_weight = face_speed * slot_live
    lower_all = face_cells[0]
    upper_all = face_cells[1]
    table = halo_blocks[0]
    ext_cells = cdev + 256 * table.shape[1]
    own_hot = (jnp.arange(cdev, dtype=jnp.int32)[:, None] == lower_all[None, :]).astype(jnp.float32)
    up_hot = (jnp.arange(ext_cells, dtype=jnp.int32)[:, None] == upper_all[None, :]).astype(
        jnp.float32
    )
    signed_hot = own_hot - up_hot[:cdev]
    cosine = jnp.cos(theta[:, None] - face_angle[None, :]) * slot_weight[None, :]
    velocity = (group_speed[None, :, None] * cosine[:, None, :]).reshape(dloc * nfreq, fdev)
    forward = jnp.maximum(velocity, 0.0)
    backward = jnp.minimum(velocity, 0.0)
    requests = with_halo(halo_blocks, (("rows", 0),), 1, False)
    wanted_above = requests[2, 0]
    wanted_below = requests[0, 1]
    current = field
    for step in range(ITERS):
        send_up = pick_blocks(current, wanted_above)
        send_down = pick_blocks(current, wanted_below)
        from_below = from_behind(send_up, "rows", 1)
        from_above = from_behind(send_down, "rows", -1)
        extended = jnp.concatenate([current, from_below, from_above], axis=2)
        spectra = extended.reshape(dloc * nfreq, extended.shape[2])
        total = block_flux(spectra, cdev, own_hot, up_hot, signed_hot, forward, backward)
        moved = current - total.reshape(dloc, nfreq, cdev) * area_scale
        rims = with_halo(moved, (("spec", 0),), 1, True)
        before = rims[:-2]
        after = rims[2:]
        current = (
            moved
            - jnp.maximum(weight_turn, 0.0) * (moved - before)
            - jnp.minimum(weight_turn, 0.0) * (after - moved)
        )
    return current


def solution(mesh):
    return jax.shard_map(
        on_device,
        mesh=mesh,
        in_specs=(
            P("spec", None, "rows"),
            P(),
            P("rows"),
            P("rows"),
            P(None, "rows"),
            P("rows"),
            P("rows", None, None),
            P("rows"),
            P("rows"),
            P("rows"),
        ),
        out_specs=P("spec", None, "rows"),
        check_vma=False,
    )
```

profile of v0, /device:TPU:13, one launch (start us, length us, event | category | flops | bytes accessed | tf_op | source)
XLA Modules:
  0.0 219.4 jit_solution(1690691987089666603)
XLA Ops:
  0.0 3.1 %collective-permute-start.2 = (s32[1,2,2]{2,1,0:T(2,128)}, s32[1,2,2]{2,1,0:T(2,128)S(1)}, u32[]{:S(2)}, u32[]{:S(2)}) collective-permute-start(s32[1,2,2]{2,1,0:T(2,128)} %param.18), channel_id=1, source_target_pairs={{0,2},{2,4},{4,6},{6,8},{8,10},{10,12},{12,14},{14,16},{16,18},{18... | collective-permute-start | bytes 56 | tf_op jit(solution)/shard_map/ppermute | solution.py:19
  3.1 3.1 %collective-permute-start = (s32[1,2,2]{2,1,0:T(2,128)}, s32[1,2,2]{2,1,0:T(2,128)S(1)}, u32[]{:S(2)}, u32[]{:S(2)}) collective-permute-start(s32[1,2,2]{2,1,0:T(2,128)} %param.18), channel_id=1, source_target_pairs={{2,0},{4,2},{6,4},{8,6},{10,8},{12,10},{14,12},{16,14},{18,16},{20... | collective-permute-start | bytes 56 | tf_op jit(solution)/shard_map/ppermute | solution.py:20
  17.5 4.3 %collective-permute-start.3 = (f32[18,30,256]{2,1,0:T(8,128)}, f32[18,30,256]{2,1,0:T(8,128)}, u32[]{:S(2)}, u32[]{:S(2)}) collective-permute-start(f32[18,30,256]{2,1,0:T(8,128)} %reshape.109), channel_id=1, source_target_pairs={{2,0},{4,2},{6,4},{8,6},{10,8},{12,10},{14,12},{16,14},{18,16},{20... | collective-permute-start | bytes 1658888 | tf_op jit(solution)/shard_map/ppermute | solution.py:28
  27.4 4.6 %collective-permute-done.1 = f32[18,30,256]{2,1,0:T(8,128)} collective-permute-done((f32[18,30,256]{2,1,0:T(8,128)}, f32[18,30,256]{2,1,0:T(8,128)}, u32[]{:S(2)}, u32[]{:S(2)}) %collective-permute-start.1) | collective-permute-done | bytes 552992 | tf_op jit(solution)/shard_map/ppermute | solution.py:28
  32.0 15.1 %collective-permute-done.3 = f32[18,30,256]{2,1,0:T(8,128)} collective-permute-done((f32[18,30,256]{2,1,0:T(8,128)}, f32[18,30,256]{2,1,0:T(8,128)}, u32[]{:S(2)}, u32[]{:S(2)}) %collective-permute-start.3) | collective-permute-done | bytes 552992 | tf_op jit(solution)/shard_map/ppermute | solution.py:28
  47.1 2.9 %pad_maximum_fusion = f32[18,30,1024]{2,1,0:T(8,128)} fusion(f32[18,30,256]{2,1,0:T(8,128)} %collective-permute-done.3, f32[18,30,256]{2,1,0:T(8,128)} %collective-permute-done.1, f32[18,30,512]{2,1,0:T(8,128)S(1)} %copy-done.2), kind=kLoop, calls=%fused_computation.10 | loop fusion | flops 1105920 | bytes 4423680 | tf_op jit(solution)/shard_map/concatenate | solution.py:102
  50.0 3.0 %reshape.110 = f32[540,1024]{1,0:T(8,128)} reshape(f32[18,30,1024]{2,1,0:T(8,128)} %pad_maximum_fusion) | data formatting | bytes 4423680 | tf_op jit(solution)/shard_map/reshape | solution.py:103
  53.0 5.6 %fusion.2 = f32[540,1024]{1,0:T(8,128)S(1)} fusion(f32[540,1024]{1,0:T(8,128)} %reshape.110, s32[1024]{0:T(1024)S(1)} %bitcast.31), kind=kOutput, calls=%fused_computation.9 | convolution fusion | flops 6795821056 | bytes 4427776 | tf_op jit(solution)/shard_map/dot_general | solution.py:44
  60.7 4.6 %fusion.11 = f32[540,512]{1,0:T(8,128)S(1)} fusion(f32[540,1024]{1,0:T(8,128)S(1)} %fusion.2, f32[540,1024]{1,0:T(8,128)S(1)} %fusion.20, f32[540,1024]{1,0:T(8,128)S(1)} %mul.143, f32[540]{0:T(1024)S(1)} %mul.133, pred[1024,1024]{1,0:T(32,128)(4,1)S(1)} %copy-done.3, s32[1024]{0:T(1024)S(1)} %bitcast.25), kind=kOutput, calls=%fused_computation.21 | convolution fusion | flops 3402801152 | bytes 8323072 | tf_op jit(solution)/shard_map/dot_general | solution.py:48
  71.5 2.8 %reshape.112 = f32[18,30,4,128]{3,2,1,0:T(4,128)} reshape(f32[18,30,512]{2,1,0:T(8,128)} %fusion.35) | data formatting | bytes 2211840 | tf_op jit(solution)/shard_map/reshape | solution.py:33
  74.3 2.5 %copy.15 = f32[18,30,4,128]{3,1,2,0:T(8,128)} copy(f32[18,30,4,128]{3,2,1,0:T(4,128)} %reshape.112) | data formatting | bytes 2211840 | tf_op jit(solution)/shard_map/reshape | solution.py:33
  76.8 2.8 %gather_fusion.3 = f32[2,18,30,128]{3,2,1,0:T(8,128)} fusion(f32[18,30,4,128]{3,1,2,0:T(8,128)} %copy.15, s32[1024]{0:T(1024)} %copy-done.17), kind=kCustom, calls=%fused_computation.3.clone | custom fusion | bytes 1105928 | tf_op jit(solution)/shard_map/jit(_take)/gather | solution.py:34
  79.6 2.8 %gather_fusion.2 = f32[2,18,30,128]{3,2,1,0:T(8,128)} fusion(f32[18,30,4,128]{3,1,2,0:T(8,128)} %copy.15, s32[1024]{0:T(1024)} %copy-done.18), kind=kCustom, calls=%fused_computation.2.clone | custom fusion | bytes 1105928 | tf_op jit(solution)/shard_map/jit(_take)/gather | solution.py:34
  88.6 2.3 %reshape.113 = f32[18,30,256]{2,1,0:T(8,128)} reshape(f32[18,30,2,128]{3,2,1,0:T(2,128)} %copy.16) | data formatting | bytes 1105920 | tf_op jit(solution)/shard_map/reshape | solution.py:34
  92.9 4.3 %collective-permute-start.7 = (f32[18,30,256]{2,1,0:T(8,128)}, f32[18,30,256]{2,1,0:T(8,128)S(1)}, u32[]{:S(2)}, u32[]{:S(2)}) collective-permute-start(f32[18,30,256]{2,1,0:T(8,128)} %reshape.114), channel_id=1, source_target_pairs={{2,0},{4,2},{6,4},{8,6},{10,8},{12,10},{14,12},{16,14},{18,16},{20... | collective-permute-start | bytes 1658888 | tf_op jit(solution)/shard_map/ppermute | solution.py:28
  97.1 11.5 %collective-permute-done.6 = f32[18,30,256]{2,1,0:T(8,128)S(1)} collective-permute-done((f32[18,30,256]{2,1,0:T(8,128)}, f32[18,30,256]{2,1,0:T(8,128)S(1)}, u32[]{:S(2)}, u32[]{:S(2)}) %collective-permute-start.6) | collective-permute-done | bytes 552992 | tf_op jit(solution)/shard_map/ppermute | solution.py:28
  108.7 12.4 %collective-permute-done.7 = f32[18,30,256]{2,1,0:T(8,128)S(1)} collective-permute-done((f32[18,30,256]{2,1,0:T(8,128)}, f32[18,30,256]{2,1,0:T(8,128)S(1)}, u32[]{:S(2)}, u32[]{:S(2)}) %collective-permute-start.7) | collective-permute-done | bytes 552992 | tf_op jit(solution)/shard_map/ppermute | solution.py:28
  121.0 2.9 %pad_maximum_fusion.1 = f32[18,30,1024]{2,1,0:T(8,128)} fusion(f32[18,30,256]{2,1,0:T(8,128)S(1)} %collective-permute-done.7, f32[18,30,256]{2,1,0:T(8,128)S(1)} %collective-permute-done.6, f32[18,30,512]{2,1,0:T(8,128)} %fusion.35), kind=kLoop, calls=%fused_computation.11 | loop fusion | flops 1105920 | bytes 4423680 | tf_op jit(solution)/shard_map/concatenate | solution.py:102
  124.0 3.0 %reshape.115 = f32[540,1024]{1,0:T(8,128)} reshape(f32[18,30,1024]{2,1,0:T(8,128)} %pad_maximum_fusion.1) | data formatting | bytes 4423680 | tf_op jit(solution)/shard_map/reshape | solution.py:103
  126.9 5.6 %fusion.1 = f32[540,1024]{1,0:T(8,128)S(1)} fusion(f32[540,1024]{1,0:T(8,128)} %reshape.115, s32[1024]{0:T(1024)} %bitcast.32), kind=kOutput, calls=%fused_computation.8 | convolution fusion | flops 6795821056 | bytes 4427776 | tf_op jit(solution)/shard_map/dot_general | solution.py:44
  134.7 5.6 %fusion.7 = f32[540,512]{1,0:T(8,128)} fusion(f32[540,1024]{1,0:T(8,128)S(1)} %fusion.1, f32[540,1024]{1,0:T(8,128)S(1)} %fusion.19, f32[540,1024]{1,0:T(8,128)S(1)} %mul.143, f32[540]{0:T(1024)S(1)} %mul.133, pred[1024,1024]{1,0:T(32,128)(4,1)S(1)} %copy-done.4, s32[1024]{0:T(1024)S(1)} %bitcast.27), kind=kOutput, calls=%fused_computation.17 | convolution fusion | flops 3402801152 | bytes 8323072 | tf_op jit(solution)/shard_map/dot_general | solution.py:48
  140.3 2.4 %reshape.116 = f32[18,30,512]{2,1,0:T(8,128)} reshape(f32[540,512]{1,0:T(8,128)} %fusion.7) | data formatting | bytes 2211840 | tf_op jit(solution)/shard_map/reshape | solution.py:105
  148.1 2.4 %copy.19 = f32[18,30,4,128]{3,1,2,0:T(8,128)} copy(f32[18,30,4,128]{3,2,1,0:T(4,128)} %reshape.117) | data formatting | bytes 2211840 | tf_op jit(solution)/shard_map/reshape | solution.py:33
  150.5 2.8 %gather_fusion.5 = f32[2,18,30,128]{3,2,1,0:T(8,128)} fusion(f32[18,30,4,128]{3,1,2,0:T(8,128)} %copy.19, s32[1024]{0:T(1024)} %copy-done.17), kind=kCustom, calls=%fused_computation.5.clone | custom fusion | bytes 1105928 | tf_op jit(solution)/shard_map/jit(_take)/gather | solution.py:34
  153.3 2.8 %gather_fusion.4 = f32[2,18,30,128]{3,2,1,0:T(8,128)} fusion(f32[18,30,4,128]{3,1,2,0:T(8,128)} %copy.19, s32[1024]{0:T(1024)} %copy-done.18), kind=kCustom, calls=%fused_computation.4.clone | custom fusion | bytes 1105928 | tf_op jit(solution)/shard_map/jit(_take)/gather | solution.py:34
  160.1 2.5 %reshape.119 = f32[18,30,256]{2,1,0:T(8,128)} reshape(f32[18,30,2,128]{3,2,1,0:T(2,128)} %copy.22) | data formatting | bytes 1105920 | tf_op jit(solution)/shard_map/reshape | solution.py:34
  166.8 4.3 %collective-permute-start.11 = (f32[18,30,256]{2,1,0:T(8,128)}, f32[18,30,256]{2,1,0:T(8,128)S(1)}, u32[]{:S(2)}, u32[]{:S(2)}) collective-permute-start(f32[18,30,256]{2,1,0:T(8,128)} %reshape.119), channel_id=1, source_target_pairs={{2,0},{4,2},{6,4},{8,6},{10,8},{12,10},{14,12},{16,14},{18,16},{20... | collective-permute-start | bytes 1658888 | tf_op jit(solution)/shard_map/ppermute | solution.py:28
  171.1 11.5 %collective-permute-done.10 = f32[18,30,256]{2,1,0:T(8,128)S(1)} collective-permute-done((f32[18,30,256]{2,1,0:T(8,128)}, f32[18,30,256]{2,1,0:T(8,128)S(1)}, u32[]{:S(2)}, u32[]{:S(2)}) %collective-permute-start.10) | collective-permute-done | bytes 552992 | tf_op jit(solution)/shard_map/ppermute | solution.py:28
  182.6 14.1 %collective-permute-done.11 = f32[18,30,256]{2,1,0:T(8,128)S(1)} collective-permute-done((f32[18,30,256]{2,1,0:T(8,128)}, f32[18,30,256]{2,1,0:T(8,128)S(1)}, u32[]{:S(2)}, u32[]{:S(2)}) %collective-permute-start.11) | collective-permute-done | bytes 552992 | tf_op jit(solution)/shard_map/ppermute | solution.py:28
  198.4 3.0 %reshape.120 = f32[540,1024]{1,0:T(8,128)} reshape(f32[18,30,1024]{2,1,0:T(8,128)} %pad_maximum_fusion.2) | data formatting | bytes 4423680 | tf_op jit(solution)/shard_map/reshape | solution.py:103
  201.3 5.6 %fusion = f32[540,1024]{1,0:T(8,128)S(1)} fusion(f32[540,1024]{1,0:T(8,128)} %reshape.120, s32[1024]{0:T(1024)S(1)} %bitcast.33), kind=kOutput, calls=%fused_computation.7 | convolution fusion | flops 6795821056 | bytes 4427776 | tf_op jit(solution)/shard_map/dot_general | solution.py:44
  209.1 4.6 %fusion.3 = f32[540,512]{1,0:T(8,128)S(1)} fusion(f32[540,1024]{1,0:T(8,128)S(1)} %fusion, f32[540,1024]{1,0:T(8,128)S(1)} %fusion.18, f32[540,1024]{1,0:T(8,128)S(1)} %mul.143, f32[540]{0:T(1024)S(1)} %mul.133, pred[1024,1024]{1,0:T(32,128)(4,1)S(1)} %copy-done.5, s32[1024]{0:T(1024)S(1)} %bitcast.29), kind=kOutput, calls=%fused_computation.13 | convolution fusion | flops 3402801152 | bytes 8323072 | tf_op jit(solution)/shard_map/dot_general | solution.py:48
  (128 shorter events, 57.1 us)
Async XLA Ops:
  0.0 9.7 %collective-permute-start.2 = (s32[1,2,2]{2,1,0:T(2,128)}, s32[1,2,2]{2,1,0:T(2,128)S(1)}, u32[]{:S(2)}, u32[]{:S(2)}) collective-permute-start(s32[1,2,2]{2,1,0:T(2,128)} %param.18), channel_id=1, source_target_pairs={{0,2},{2,4},{4,6},{6,8},{8,10},{10,12},{12,14},{14,16},{16,18},{18... | collective-permute-start | bytes 56 | tf_op jit(solution)/shard_map/ppermute | solution.py:19
  3.1 6.6 %collective-permute-start = (s32[1,2,2]{2,1,0:T(2,128)}, s32[1,2,2]{2,1,0:T(2,128)S(1)}, u32[]{:S(2)}, u32[]{:S(2)}) collective-permute-start(s32[1,2,2]{2,1,0:T(2,128)} %param.18), channel_id=1, source_target_pairs={{2,0},{4,2},{6,4},{8,6},{10,8},{12,10},{14,12},{16,14},{18,16},{20... | collective-permute-start | bytes 56 | tf_op jit(solution)/shard_map/ppermute | solution.py:20
  9.7 2.4 %copy-start.19 = (pred[2]{0:T(512)(128)(4,1)}, pred[2]{0:T(512)(128)(4,1)S(1)}, u32[]{:S(2)}) copy-start(pred[2]{0:T(512)(128)(4,1)S(1)} %get-tuple-element.8) | copy-start | bytes 10
  12.7 9.2 %copy-start.26 = (s32[512]{0:T(512)S(1)}, s32[512]{0:T(512)}, u32[]{:S(2)}) copy-start(s32[512]{0:T(512)} %param.19) | copy-start | bytes 6148
  12.7 9.2 %copy-start.29 = (f32[30]{0:T(128)S(1)}, f32[30]{0:T(128)}, u32[]{:S(2)}) copy-start(f32[30]{0:T(128)} %param.13) | copy-start | bytes 364
  15.2 16.7 %collective-permute-start.1 = (f32[18,30,256]{2,1,0:T(8,128)}, f32[18,30,256]{2,1,0:T(8,128)}, u32[]{:S(2)}, u32[]{:S(2)}) collective-permute-start(f32[18,30,256]{2,1,0:T(8,128)} %reshape.108), channel_id=1, source_target_pairs={{0,2},{2,4},{4,6},{6,8},{8,10},{10,12},{12,14},{14,16},{16,18},{18... | collective-permute-start | bytes 1658888 | tf_op jit(solution)/shard_map/ppermute | solution.py:28
  17.5 29.5 %collective-permute-start.3 = (f32[18,30,256]{2,1,0:T(8,128)}, f32[18,30,256]{2,1,0:T(8,128)}, u32[]{:S(2)}, u32[]{:S(2)}) collective-permute-start(f32[18,30,256]{2,1,0:T(8,128)} %reshape.109), channel_id=1, source_target_pairs={{2,0},{4,2},{6,4},{8,6},{10,8},{12,10},{14,12},{16,14},{18,16},{20... | collective-permute-start | bytes 1658888 | tf_op jit(solution)/shard_map/ppermute | solution.py:28
  21.9 44.5 %copy-start.12 = (f32[512]{0:T(512)}, f32[512]{0:T(512)S(1)}, u32[]{:S(2)}) copy-start(f32[512]{0:T(512)S(1)} %multiply_exponential_fusion) | copy-start | bytes 6148
  23.7 23.3 %copy-start.2 = (f32[18,30,512]{2,1,0:T(8,128)S(1)}, f32[18,30,512]{2,1,0:T(8,128)}, u32[]{:S(2)}) copy-start(f32[18,30,512]{2,1,0:T(8,128)} %param.12) | copy-start | bytes 3317764
  25.6 27.4 %copy-start.14 = (s32[1,1024]{1,0:T(1,128)}, s32[1,1024]{1,0:T(1,128)S(1)}, u32[]{:S(2)}) copy-start(s32[1,1024]{1,0:T(1,128)S(1)} %get-tuple-element.17) | copy-start | bytes 12292
  53.0 5.6 %copy-start.6 = (f32[540,1024]{1,0:T(8,128)S(1)}, f32[540,1024]{1,0:T(8,128)}, u32[]{:S(2)}) copy-start(f32[540,1024]{1,0:T(8,128)} %reshape.110) | copy-start | bytes 6635524
  66.5 2.6 %copy-start.27 = (f32[512]{0:T(512)S(1)}, f32[512]{0:T(512)}, u32[]{:S(2)}) copy-start(f32[512]{0:T(512)} %param.21) | copy-start | bytes 6148
  66.5 2.6 %copy-start.28 = (s32[512]{0:T(512)S(1)}, s32[512]{0:T(512)}, u32[]{:S(2)}) copy-start(s32[512]{0:T(512)} %param.20) | copy-start | bytes 6148
  68.4 1.5 collective-permute-start.4
  69.0 1.3 collective-permute-start.5
  82.4 2.5 %copy-start.10 = (f32[2,18,30,128]{3,2,1,0:T(8,128)S(1)}, f32[2,18,30,128]{3,2,1,0:T(8,128)}, u32[]{:S(2)}) copy-start(f32[2,18,30,128]{3,2,1,0:T(8,128)} %gather_fusion.3) | copy-start | bytes 1658884
  82.4 2.5 %copy-start.20 = (pred[2]{0:T(512)(128)(4,1)S(1)}, pred[2]{0:T(512)(128)(4,1)}, u32[]{:S(2)}) copy-start(pred[2]{0:T(512)(128)(4,1)} %copy-done.19) | copy-start | bytes 10
  91.0 17.7 %collective-permute-start.6 = (f32[18,30,256]{2,1,0:T(8,128)}, f32[18,30,256]{2,1,0:T(8,128)S(1)}, u32[]{:S(2)}, u32[]{:S(2)}) collective-permute-start(f32[18,30,256]{2,1,0:T(8,128)} %reshape.113), channel_id=1, source_target_pairs={{0,2},{2,4},{4,6},{6,8},{8,10},{10,12},{12,14},{14,16},{16,18},{18... | collective-permute-start | bytes 1658888 | tf_op jit(solution)/shard_map/ppermute | solution.py:28
  92.9 28.2 %collective-permute-start.7 = (f32[18,30,256]{2,1,0:T(8,128)}, f32[18,30,256]{2,1,0:T(8,128)S(1)}, u32[]{:S(2)}, u32[]{:S(2)}) collective-permute-start(f32[18,30,256]{2,1,0:T(8,128)} %reshape.114), channel_id=1, source_target_pairs={{2,0},{4,2},{6,4},{8,6},{10,8},{12,10},{14,12},{16,14},{18,16},{20... | collective-permute-start | bytes 1658888 | tf_op jit(solution)/shard_map/ppermute | solution.py:28
  126.9 5.6 %copy-start.8 = (f32[540,1024]{1,0:T(8,128)S(1)}, f32[540,1024]{1,0:T(8,128)}, u32[]{:S(2)}) copy-start(f32[540,1024]{1,0:T(8,128)} %reshape.115) | copy-start | bytes 6635524
  144.3 1.4 collective-permute-start.8
  144.8 1.3 collective-permute-start.9
  150.5 5.6 %copy-start.23 = (pred[2]{0:T(512)(128)(4,1)S(1)}, pred[2]{0:T(512)(128)(4,1)}, u32[]{:S(2)}) copy-start(pred[2]{0:T(512)(128)(4,1)} %copy-done.22) | copy-start | bytes 10
  156.2 2.5 %copy-start.9 = (f32[2,18,30,128]{3,2,1,0:T(8,128)S(1)}, f32[2,18,30,128]{3,2,1,0:T(8,128)}, u32[]{:S(2)}) copy-start(f32[2,18,30,128]{3,2,1,0:T(8,128)} %gather_fusion.5) | copy-start | bytes 1658884
  156.2 2.5 %copy-start.21 = (pred[2]{0:T(512)(128)(4,1)S(1)}, pred[2]{0:T(512)(128)(4,1)}, u32[]{:S(2)}) copy-start(pred[2]{0:T(512)(128)(4,1)} %copy-done.19) | copy-start | bytes 10
  164.9 17.7 %collective-permute-start.10 = (f32[18,30,256]{2,1,0:T(8,128)}, f32[18,30,256]{2,1,0:T(8,128)S(1)}, u32[]{:S(2)}, u32[]{:S(2)}) collective-permute-start(f32[18,30,256]{2,1,0:T(8,128)} %reshape.118), channel_id=1, source_target_pairs={{0,2},{2,4},{4,6},{6,8},{8,10},{10,12},{12,14},{14,16},{16,18},{18... | collective-permute-start | bytes 1658888 | tf_op jit(solution)/shard_map/ppermute | solution.py:28
  166.8 29.9 %collective-permute-start.11 = (f32[18,30,256]{2,1,0:T(8,128)}, f32[18,30,256]{2,1,0:T(8,128)S(1)}, u32[]{:S(2)}, u32[]{:S(2)}) collective-permute-start(f32[18,30,256]{2,1,0:T(8,128)} %reshape.119), channel_id=1, source_target_pairs={{2,0},{4,2},{6,4},{8,6},{10,8},{12,10},{14,12},{16,14},{18,16},{20... | collective-permute-start | bytes 1658888 | tf_op jit(solution)/shard_map/ppermute | solution.py:28
  198.3 3.0 %copy-start.15 = (s32[1,1024]{1,0:T(1,128)S(1)}, s32[1,1024]{1,0:T(1,128)}, u32[]{:S(2)}) copy-start(s32[1,1024]{1,0:T(1,128)} %copy-done.14) | copy-start | bytes 12292
  201.3 5.6 %copy-start.7 = (f32[540,1024]{1,0:T(8,128)S(1)}, f32[540,1024]{1,0:T(8,128)}, u32[]{:S(2)}) copy-start(f32[540,1024]{1,0:T(8,128)} %reshape.120) | copy-start | bytes 6635524
  207.0 2.1 copy-start.5
  216.1 1.4 collective-permute-start.12
  216.6 1.3 collective-permute-start.13
  (12 other events, 16.2 us)
where the time goes:
time: 224 us; the launch traced here: 219 us
  waiting for transfers between devices  72.7 us (32%)
  local copies, waits for them, and re-layouts  60 us (27%)
  matrix products  37.9 us (17%)
  starting transfers between devices  27 us (12%)
  other arithmetic  20.3 us (9%)
    ppermute x6, waiting for transfers between devices, from_behind(): lax.ppermute(value, axis, [(source, source + steps) for source in range(f...  69.2 us
    ppermute x6, starting transfers between devices, from_behind(): lax.ppermute(value, axis, [(source, source + steps) for source in range(f...  19 us
    dot_general x3, matrix products, block_flux(): jnp.dot(spectra, up_hot, precision=lax.Precision.HIGHEST, preferred_eleme...  16.9 us
    dot_general x3, matrix products, block_flux(): lax.dot_general(flux, signed_hot, (((1,), (1,)), ((), ())), precision=lax...  14.8 us
    gather x6, local copies, waits for them, and re-layouts, pick_blocks(): return jnp.take(view, table, axis=2).reshape(ndir, nfreq, -1)  12.4 us
    reshape x6, local copies, waits for them, and re-layouts, pick_blocks(): return jnp.take(view, table, axis=2).reshape(ndir, nfreq, -1)  12 us
    reshape x6, local copies, waits for them, and re-layouts, pick_blocks(): view = neighbour.reshape(ndir, nfreq, cdev // 128, 128)  10.9 us
    reshape x3, local copies, waits for them, and re-layouts, on_device(): spectra = extended.reshape(dloc * nfreq, extended.shape[2])  8.88 us
  transfers between devices with their start and end apart: 14, of which 12 were waited for; matrix products, arithmetic and copies ran while one was open for 4% of the time, Pallas kernels for 0%

commit v1 on v0

--- a/solution.py
+++ b/solution.py
@@ -34,24 +34,23 @@
     return jnp.take(view, table, axis=2).reshape(ndir, nfreq, -1)
 
 
+def split(x):
+    high = x.astype(jnp.bfloat16)
+    low = (x - high.astype(jnp.float32)).astype(jnp.bfloat16)
+    return jnp.concatenate([high, low], axis=1)
+
+
+def pieces_dot(x, hot, contract):
+    return lax.dot_general(
+        split(x), hot, (((1,), (contract,)), ((), ())), preferred_element_type=jnp.float32
+    )
+
+
 def block_flux(spectra, own_cells, own_hot, up_hot, signed_hot, forward, backward):
-    low_vals = jnp.dot(
-        spectra[:, :own_cells],
-        own_hot,
-        precision=lax.Precision.HIGHEST,
-        preferred_element_type=jnp.float32,
-    )
-    up_vals = jnp.dot(
-        spectra, up_hot, precision=lax.Precision.HIGHEST, preferred_element_type=jnp.float32
-    )
+    low_vals = pieces_dot(spectra[:, :own_cells], own_hot, 0)
+    up_vals = pieces_dot(spectra, up_hot, 0)
     flux = forward * low_vals + backward * up_vals
-    return lax.dot_general(
-        flux,
-        signed_hot,
-        (((1,), (1,)), ((), ())),
-        precision=lax.Precision.HIGHEST,
-        preferred_element_type=jnp.float32,
-    )
+    return pieces_dot(flux, signed_hot, 1)
 
 
 def on_device(
@@ -86,6 +85,9 @@
         jnp.float32
     )
     signed_hot = own_hot - up_hot[:cdev]
+    own_twice = jnp.concatenate([own_hot, own_hot], axis=0).astype(jnp.bfloat16)
+    up_twice = jnp.concatenate([up_hot, up_hot], axis=0).astype(jnp.bfloat16)
+    signed_twice = jnp.concatenate([signed_hot, signed_hot], axis=1).astype(jnp.bfloat16)
     cosine = jnp.cos(theta[:, None] - face_angle[None, :]) * slot_weight[None, :]
     velocity = (group_speed[None, :, None] * cosine[:, None, :]).reshape(dloc * nfreq, fdev)
     forward = jnp.maximum(velocity, 0.0)
@@ -101,7 +103,9 @@
         from_above = from_behind(send_down, "rows", -1)
         extended = jnp.concatenate([current, from_below, from_above], axis=2)
         spectra = extended.reshape(dloc * nfreq, extended.shape[2])
-        total = block_flux(spectra, cdev, own_hot, up_hot, signed_hot, forward, backward)
+        total = block_flux(
+            spectra, cdev, own_twice, up_twice, signed_twice, forward, backward
+        )
         moved = current - total.reshape(dloc, nfreq, cdev) * area_scale
         rims = with_halo(moved, (("spec", 0),), 1, True)
         before = rims[:-2]

time: 224 us -> 179 us (0.80); the launches traced: 219 us -> 178 us
  local copies, waits for them, and re-layouts: 60 us -> 35.9 us
  matrix products: 37.9 us -> 16.4 us
  other arithmetic: 20.3 us -> 23.3 us
    dot_general x9, matrix products: 37.9 us -> 16.4 us  [pieces_dot(): lax.dot_general(split(x), hot, (((1,), (contract,)), ((), ())), preferred...]
    reshape x6, local copies, waits for them, and re-layouts: 12 us -> 3.48 us  [pick_blocks(): return jnp.take(view, table, axis=2).reshape(ndir, nfreq, -1)]
    unnamed x60 -> x68, local copies, waits for them, and re-layouts: 2.68 us -> 9.69 us
    gather x6, local copies, waits for them, and re-layouts: 12.4 us -> 5.39 us  [pick_blocks(): return jnp.take(view, table, axis=2).reshape(ndir, nfreq, -1)]
    reshape x6, local copies, waits for them, and re-layouts: 10.9 us -> 5.21 us  [pick_blocks(): view = neighbour.reshape(ndir, nfreq, cdev // 128, 128)]
    convert_element_type x0 -> x7, other arithmetic: none -> 5.24 us  [the longest x1 3.47 us: on_device(): (jnp.arange(ext_cells, dtype=jnp.int32)[:, None] == upper_all[None, :]).a...]
    reshape x3, local copies, waits for them, and re-layouts: 8.88 us -> 5.13 us  [on_device(): spectra = extended.reshape(dloc * nfreq, extended.shape[2])]
    reshape x3, local copies, waits for them, and re-layouts: 3.65 us -> 0.39 us  [on_device(): moved = current - total.reshape(dloc, nfreq, cdev) * area_scale]
  transfers between devices with their start and end apart: 14 -> 14, of which waited for: 12 -> 12; matrix products, arithmetic and copies ran while one was open for 4% -> 8% of each run, Pallas kernels for 0% -> 0%
where the time goes in v1:
time: 179 us; the launch traced here: 178 us
  waiting for transfers between devices  74 us (41%)
  local copies, waits for them, and re-layouts  35.9 us (20%)
  starting transfers between devices  27.2 us (15%)
  other arithmetic  23.3 us (13%)
  matrix products  16.4 us (9%)
    ppermute x6, waiting for transfers between devices, from_behind(): lax.ppermute(value, axis, [(source, source + steps) for source in range(f...  70.5 us
    ppermute x6, starting transfers between devices, from_behind(): lax.ppermute(value, axis, [(source, source + steps) for source in range(f...  19.2 us
    dot_general x9, matrix products, pieces_dot(): lax.dot_general(split(x), hot, (((1,), (contract,)), ((), ())), preferred...  16.4 us
    unnamed x68, local copies, waits for them, and re-layouts  9.69 us
    gather x6, local copies, waits for them, and re-layouts, pick_blocks(): return jnp.take(view, table, axis=2).reshape(ndir, nfreq, -1)  5.39 us
    reshape x6, local copies, waits for them, and re-layouts, pick_blocks(): view = neighbour.reshape(ndir, nfreq, cdev // 128, 128)  5.21 us
    reshape x3, local copies, waits for them, and re-layouts, on_device(): spectra = extended.reshape(dloc * nfreq, extended.shape[2])  5.13 us
    concatenate x3, other arithmetic, on_device(): extended = jnp.concatenate([current, from_below, from_above], axis=2)  5.05 us
  transfers between devices with their start and end apart: 14, of which 12 were waited for; matrix products, arithmetic and copies ran while one was open for 8% of the time, Pallas kernels for 0%

profile of v1, /device:TPU:13, one launch (start us, length us, event | category | flops | bytes accessed | tf_op | source)
XLA Modules:
  0.0 178.3 jit_solution(12492011527778874695)
XLA Ops:
  0.0 3.1 %collective-permute-start.2 = (s32[1,2,2]{2,1,0:T(2,128)}, s32[1,2,2]{2,1,0:T(2,128)}, u32[]{:S(2)}, u32[]{:S(2)}) collective-permute-start(s32[1,2,2]{2,1,0:T(2,128)} %param.18), channel_id=1, source_target_pairs={{0,2},{2,4},{4,6},{6,8},{8,10},{10,12},{12,14},{14,16},{16,18},{18... | collective-permute-start | bytes 56 | tf_op jit(solution)/shard_map/ppermute | solution.py:19
  3.1 3.1 %collective-permute-start = (s32[1,2,2]{2,1,0:T(2,128)}, s32[1,2,2]{2,1,0:T(2,128)}, u32[]{:S(2)}, u32[]{:S(2)}) collective-permute-start(s32[1,2,2]{2,1,0:T(2,128)} %param.18), channel_id=1, source_target_pairs={{2,0},{4,2},{6,4},{8,6},{10,8},{12,10},{14,12},{16,14},{18,16},{20... | collective-permute-start | bytes 56 | tf_op jit(solution)/shard_map/ppermute | solution.py:20
  9.7 1.7 reshape.107
  12.3 1.7 mul.143
  13.9 3.5 %fusion = (f32[1024,1024]{1,0:T(8,128)}, bf16[1024,1024]{1,0:T(8,128)(2,1)}) fusion(s32[1024]{0:T(1024)S(1)} %bitcast.23), kind=kLoop, calls=%fused_computation.8 | loop fusion | flops 3145728 | bytes 6295552 | tf_op jit(solution)/shard_map/convert_element_type | solution.py:84
  22.0 2.2 %collective-permute-start.1 = (f32[18,30,256]{2,1,0:T(8,128)S(1)}, f32[18,30,256]{2,1,0:T(8,128)S(1)}, u32[]{:S(2)}, u32[]{:S(2)}) collective-permute-start(f32[18,30,256]{2,1,0:T(8,128)S(1)} %reshape.108), channel_id=1, source_target_pairs={{0,2},{2,4},{4,6},{6,8},{8,10},{10,12},{12,14},{14,16},{16,18},{18... | collective-permute-start | bytes 1658888 | tf_op jit(solution)/shard_map/ppermute | solution.py:28
  24.3 4.1 %collective-permute-start.3 = (f32[18,30,256]{2,1,0:T(8,128)S(1)}, f32[18,30,256]{2,1,0:T(8,128)S(1)}, u32[]{:S(2)}, u32[]{:S(2)}) collective-permute-start(f32[18,30,256]{2,1,0:T(8,128)S(1)} %reshape.109), channel_id=1, source_target_pairs={{2,0},{4,2},{6,4},{8,6},{10,8},{12,10},{14,12},{16,14},{18,16},{20... | collective-permute-start | bytes 1658888 | tf_op jit(solution)/shard_map/ppermute | solution.py:28
  29.7 1.9 %fusion.25 = bf16[512,1024]{1,0:T(8,128)(2,1)S(1)} fusion(f32[1024,1024]{1,0:T(8,128)} %get-tuple-element.38, s32[1024]{0:T(1024)S(1)} %bitcast.22), kind=kLoop, calls=%fused_computation.47 | loop fusion | flops 2097152 | bytes 3149824 | tf_op jit(solution)/shard_map/convert
  31.6 6.8 %collective-permute-done.1 = f32[18,30,256]{2,1,0:T(8,128)S(1)} collective-permute-done((f32[18,30,256]{2,1,0:T(8,128)S(1)}, f32[18,30,256]{2,1,0:T(8,128)S(1)}, u32[]{:S(2)}, u32[]{:S(2)}) %collective-permute-start.1) | collective-permute-done | bytes 552992 | tf_op jit(solution)/shard_map/ppermute | solution.py:28
  38.5 15.1 %collective-permute-done.3 = f32[18,30,256]{2,1,0:T(8,128)S(1)} collective-permute-done((f32[18,30,256]{2,1,0:T(8,128)S(1)}, f32[18,30,256]{2,1,0:T(8,128)S(1)}, u32[]{:S(2)}, u32[]{:S(2)}) %collective-permute-start.3) | collective-permute-done | bytes 552992 | tf_op jit(solution)/shard_map/ppermute | solution.py:28
  53.6 1.7 pad_maximum_fusion.4
  55.2 1.7 reshape.110
  60.6 2.8 %subtract_convert_fusion.4 = (bf16[540,1024]{1,0:T(8,128)(2,1)S(1)}, bf16[540,1024]{1,0:T(8,128)(2,1)S(1)}) fusion(bf16[1024,1024]{1,0:T(8,128)(2,1)S(1)} %copy-done.8, bf16[540,1024]{1,0:T(8,128)(2,1)S(1)} %get-tuple-element.20, bf16[540,1024]{1,0:T(8,128)(2,1)S(1)} %get-tuple-element.21, f32[540,1024]{1,0:T(8,128)S(1)} %fusion.28, ...), kind=kOutput, calls=%fused_computation.44 | convolution fusion | flops 2283266048 | bytes 10946672 | tf_op jit(solution)/shard_map/dot_general | solution.py:44
  69.0 1.4 reshape.112
  70.4 1.4 copy.15
  71.8 1.4 gather_fusion.3
  73.2 1.5 gather_fusion.2
  79.3 1.9 %collective-permute-start.6 = (f32[18,30,256]{2,1,0:T(8,128)S(1)}, f32[18,30,256]{2,1,0:T(8,128)S(1)}, u32[]{:S(2)}, u32[]{:S(2)}) collective-permute-start(f32[18,30,256]{2,1,0:T(8,128)S(1)} %reshape.113), channel_id=1, source_target_pairs={{0,2},{2,4},{4,6},{6,8},{8,10},{10,12},{12,14},{14,16},{16,18},{18... | collective-permute-start | bytes 1658888 | tf_op jit(solution)/shard_map/ppermute | solution.py:28
  81.3 4.5 %collective-permute-start.7 = (f32[18,30,256]{2,1,0:T(8,128)}, f32[18,30,256]{2,1,0:T(8,128)S(1)}, u32[]{:S(2)}, u32[]{:S(2)}) collective-permute-start(f32[18,30,256]{2,1,0:T(8,128)} %reshape.114), channel_id=1, source_target_pairs={{2,0},{4,2},{6,4},{8,6},{10,8},{12,10},{14,12},{16,14},{18,16},{20... | collective-permute-start | bytes 1658888 | tf_op jit(solution)/shard_map/ppermute | solution.py:28
  85.8 11.1 %collective-permute-done.6 = f32[18,30,256]{2,1,0:T(8,128)S(1)} collective-permute-done((f32[18,30,256]{2,1,0:T(8,128)S(1)}, f32[18,30,256]{2,1,0:T(8,128)S(1)}, u32[]{:S(2)}, u32[]{:S(2)}) %collective-permute-start.6) | collective-permute-done | bytes 552992 | tf_op jit(solution)/shard_map/ppermute | solution.py:28
  96.9 12.4 %collective-permute-done.7 = f32[18,30,256]{2,1,0:T(8,128)S(1)} collective-permute-done((f32[18,30,256]{2,1,0:T(8,128)}, f32[18,30,256]{2,1,0:T(8,128)S(1)}, u32[]{:S(2)}, u32[]{:S(2)}) %collective-permute-start.7) | collective-permute-done | bytes 552992 | tf_op jit(solution)/shard_map/ppermute | solution.py:28
  109.2 1.7 pad_maximum_fusion.5
  110.9 1.7 reshape.115
  116.3 2.8 %subtract_convert_fusion.2 = (bf16[540,1024]{1,0:T(8,128)(2,1)S(1)}, bf16[540,1024]{1,0:T(8,128)(2,1)S(1)}) fusion(bf16[1024,1024]{1,0:T(8,128)(2,1)S(1)} %copy-done.9, bf16[540,1024]{1,0:T(8,128)(2,1)S(1)} %get-tuple-element.14, bf16[540,1024]{1,0:T(8,128)(2,1)S(1)} %get-tuple-element.15, f32[540,1024]{1,0:T(8,128)S(1)} %fusion.27, ...), kind=kOutput, calls=%fused_computation.41 | convolution fusion | flops 2283266048 | bytes 10946672 | tf_op jit(solution)/shard_map/dot_general | solution.py:44
  129.9 1.9 %collective-permute-start.10 = (f32[18,30,256]{2,1,0:T(8,128)S(1)}, f32[18,30,256]{2,1,0:T(8,128)S(1)}, u32[]{:S(2)}, u32[]{:S(2)}) collective-permute-start(f32[18,30,256]{2,1,0:T(8,128)S(1)} %reshape.118), channel_id=1, source_target_pairs={{0,2},{2,4},{4,6},{6,8},{8,10},{10,12},{12,14},{14,16},{16,18},{18... | collective-permute-start | bytes 1658888 | tf_op jit(solution)/shard_map/ppermute | solution.py:28
  131.8 4.5 %collective-permute-start.11 = (f32[18,30,256]{2,1,0:T(8,128)S(1)}, f32[18,30,256]{2,1,0:T(8,128)S(1)}, u32[]{:S(2)}, u32[]{:S(2)}) collective-permute-start(f32[18,30,256]{2,1,0:T(8,128)S(1)} %reshape.119), channel_id=1, source_target_pairs={{2,0},{4,2},{6,4},{8,6},{10,8},{12,10},{14,12},{16,14},{18,16},{20... | collective-permute-start | bytes 1658888 | tf_op jit(solution)/shard_map/ppermute | solution.py:28
  136.4 10.9 %collective-permute-done.10 = f32[18,30,256]{2,1,0:T(8,128)S(1)} collective-permute-done((f32[18,30,256]{2,1,0:T(8,128)S(1)}, f32[18,30,256]{2,1,0:T(8,128)S(1)}, u32[]{:S(2)}, u32[]{:S(2)}) %collective-permute-start.10) | collective-permute-done | bytes 552992 | tf_op jit(solution)/shard_map/ppermute | solution.py:28
  147.2 14.2 %collective-permute-done.11 = f32[18,30,256]{2,1,0:T(8,128)S(1)} collective-permute-done((f32[18,30,256]{2,1,0:T(8,128)S(1)}, f32[18,30,256]{2,1,0:T(8,128)S(1)}, u32[]{:S(2)}, u32[]{:S(2)}) %collective-permute-start.11) | collective-permute-done | bytes 552992 | tf_op jit(solution)/shard_map/ppermute | solution.py:28
  161.5 1.7 pad_maximum_fusion.6
  163.1 1.7 reshape.120
  168.5 2.8 %subtract_convert_fusion = (bf16[540,1024]{1,0:T(8,128)(2,1)S(1)}, bf16[540,1024]{1,0:T(8,128)(2,1)S(1)}) fusion(bf16[1024,1024]{1,0:T(8,128)(2,1)S(1)} %copy-done.10, bf16[540,1024]{1,0:T(8,128)(2,1)S(1)} %get-tuple-element.8, bf16[540,1024]{1,0:T(8,128)(2,1)S(1)} %get-tuple-element.9, f32[540,1024]{1,0:T(8,128)S(1)} %fusion.26, ...), kind=kOutput, calls=%fused_computation.38 | convolution fusion | flops 2283266048 | bytes 10946672 | tf_op jit(solution)/shard_map/dot_general | solution.py:44
  171.3 1.4 fusion.21
  (144 shorter events, 46.6 us)
Async XLA Ops:
  0.0 17.4 %collective-permute-start.2 = (s32[1,2,2]{2,1,0:T(2,128)}, s32[1,2,2]{2,1,0:T(2,128)}, u32[]{:S(2)}, u32[]{:S(2)}) collective-permute-start(s32[1,2,2]{2,1,0:T(2,128)} %param.18), channel_id=1, source_target_pairs={{0,2},{2,4},{4,6},{6,8},{8,10},{10,12},{12,14},{14,16},{16,18},{18... | collective-permute-start | bytes 56 | tf_op jit(solution)/shard_map/ppermute | solution.py:19
  3.1 14.9 %collective-permute-start = (s32[1,2,2]{2,1,0:T(2,128)}, s32[1,2,2]{2,1,0:T(2,128)}, u32[]{:S(2)}, u32[]{:S(2)}) collective-permute-start(s32[1,2,2]{2,1,0:T(2,128)} %param.18), channel_id=1, source_target_pairs={{2,0},{4,2},{6,4},{8,6},{10,8},{12,10},{14,12},{16,14},{18,16},{20... | collective-permute-start | bytes 56 | tf_op jit(solution)/shard_map/ppermute | solution.py:20
  9.7 1.9 %copy-start.27 = (f32[1024]{0:T(1024)S(1)}, f32[1024]{0:T(1024)}, u32[]{:S(2)}) copy-start(f32[1024]{0:T(1024)} %param.15) | copy-start | bytes 12292
  9.7 1.9 %copy-start.31 = (f32[1024]{0:T(1024)S(1)}, f32[1024]{0:T(1024)}, u32[]{:S(2)}) copy-start(f32[1024]{0:T(1024)} %param.14) | copy-start | bytes 12292
  18.0 2.5 %copy-start.24 = (pred[2]{0:T(512)(128)(4,1)}, pred[2]{0:T(512)(128)(4,1)S(1)}, u32[]{:S(2)}) copy-start(pred[2]{0:T(512)(128)(4,1)S(1)} %get-tuple-element.26) | copy-start | bytes 10
  18.7 1.8 %copy-start.26 = (pred[2]{0:T(512)(128)(4,1)}, pred[2]{0:T(512)(128)(4,1)S(1)}, u32[]{:S(2)}) copy-start(pred[2]{0:T(512)(128)(4,1)S(1)} %get-tuple-element.24) | copy-start | bytes 10
  18.7 1.8 %copy-start.23 = (s32[1024]{0:T(1024)}, s32[1024]{0:T(1024)S(1)}, u32[]{:S(2)}) copy-start(s32[1024]{0:T(1024)S(1)} %pad_clamp_fusion.1) | copy-start | bytes 12292
  22.0 16.4 %collective-permute-start.1 = (f32[18,30,256]{2,1,0:T(8,128)S(1)}, f32[18,30,256]{2,1,0:T(8,128)S(1)}, u32[]{:S(2)}, u32[]{:S(2)}) collective-permute-start(f32[18,30,256]{2,1,0:T(8,128)S(1)} %reshape.108), channel_id=1, source_target_pairs={{0,2},{2,4},{4,6},{6,8},{8,10},{10,12},{12,14},{14,16},{16,18},{18... | collective-permute-start | bytes 1658888 | tf_op jit(solution)/shard_map/ppermute | solution.py:28
  24.3 29.3 %collective-permute-start.3 = (f32[18,30,256]{2,1,0:T(8,128)S(1)}, f32[18,30,256]{2,1,0:T(8,128)S(1)}, u32[]{:S(2)}, u32[]{:S(2)}) collective-permute-start(f32[18,30,256]{2,1,0:T(8,128)S(1)} %reshape.109), channel_id=1, source_target_pairs={{2,0},{4,2},{6,4},{8,6},{10,8},{12,10},{14,12},{16,14},{18,16},{20... | collective-permute-start | bytes 1658888 | tf_op jit(solution)/shard_map/ppermute | solution.py:28
  28.4 25.1 %copy-start.2 = (f32[18,30,512]{2,1,0:T(8,128)S(1)}, f32[18,30,512]{2,1,0:T(8,128)}, u32[]{:S(2)}) copy-start(f32[18,30,512]{2,1,0:T(8,128)} %param.12) | copy-start | bytes 3317764
  31.6 31.8 %copy-start.11 = (bf16[512,1024]{1,0:T(8,128)(2,1)}, bf16[512,1024]{1,0:T(8,128)(2,1)S(1)}, u32[]{:S(2)}) copy-start(bf16[512,1024]{1,0:T(8,128)(2,1)S(1)} %fusion.25) | copy-start | bytes 3145732
  58.3 2.3 %copy-start.8 = (bf16[1024,1024]{1,0:T(8,128)(2,1)S(1)}, bf16[1024,1024]{1,0:T(8,128)(2,1)}, u32[]{:S(2)}) copy-start(bf16[1024,1024]{1,0:T(8,128)(2,1)} %get-tuple-element.39) | copy-start | bytes 6291460
  58.3 2.3 %copy-start.28 = (f32[540]{0:T(1024)S(1)}, f32[540]{0:T(1024)}, u32[]{:S(2)}) copy-start(f32[540]{0:T(1024)} %mul.133) | copy-start | bytes 6484
  66.3 1.5 collective-permute-start.4
  66.9 1.3 collective-permute-start.5
  74.7 1.7 copy-start.7
  79.3 17.5 %collective-permute-start.6 = (f32[18,30,256]{2,1,0:T(8,128)S(1)}, f32[18,30,256]{2,1,0:T(8,128)S(1)}, u32[]{:S(2)}, u32[]{:S(2)}) collective-permute-start(f32[18,30,256]{2,1,0:T(8,128)S(1)} %reshape.113), channel_id=1, source_target_pairs={{0,2},{2,4},{4,6},{6,8},{8,10},{10,12},{12,14},{14,16},{16,18},{18... | collective-permute-start | bytes 1658888 | tf_op jit(solution)/shard_map/ppermute | solution.py:28
  81.3 28.0 %collective-permute-start.7 = (f32[18,30,256]{2,1,0:T(8,128)}, f32[18,30,256]{2,1,0:T(8,128)S(1)}, u32[]{:S(2)}, u32[]{:S(2)}) collective-permute-start(f32[18,30,256]{2,1,0:T(8,128)} %reshape.114), channel_id=1, source_target_pairs={{2,0},{4,2},{6,4},{8,6},{10,8},{12,10},{14,12},{16,14},{18,16},{20... | collective-permute-start | bytes 1658888 | tf_op jit(solution)/shard_map/ppermute | solution.py:28
  114.0 2.3 %copy-start.9 = (bf16[1024,1024]{1,0:T(8,128)(2,1)S(1)}, bf16[1024,1024]{1,0:T(8,128)(2,1)}, u32[]{:S(2)}) copy-start(bf16[1024,1024]{1,0:T(8,128)(2,1)} %get-tuple-element.39) | copy-start | bytes 6291460
  114.0 2.3 %copy-start.29 = (f32[540]{0:T(1024)S(1)}, f32[540]{0:T(1024)}, u32[]{:S(2)}) copy-start(f32[540]{0:T(1024)} %mul.133) | copy-start | bytes 6484
  116.3 2.8 %copy-start.12 = (bf16[512,1024]{1,0:T(8,128)(2,1)S(1)}, bf16[512,1024]{1,0:T(8,128)(2,1)}, u32[]{:S(2)}) copy-start(bf16[512,1024]{1,0:T(8,128)(2,1)} %copy-done.11) | copy-start | bytes 3145732
  122.5 1.8 %copy-start = (f32[18,30,512]{2,1,0:T(8,128)}, f32[18,30,512]{2,1,0:T(8,128)S(1)}, u32[]{:S(2)}) copy-start(f32[18,30,512]{2,1,0:T(8,128)S(1)} %multiply_subtract_fusion.1) | copy-start | bytes 3317764
  122.5 1.4 collective-permute-start.8
  123.0 1.3 collective-permute-start.9
  126.5 1.9 %copy-start.25 = (pred[2]{0:T(512)(128)(4,1)S(1)}, pred[2]{0:T(512)(128)(4,1)}, u32[]{:S(2)}) copy-start(pred[2]{0:T(512)(128)(4,1)} %copy-done.24) | copy-start | bytes 10
  129.9 17.3 %collective-permute-start.10 = (f32[18,30,256]{2,1,0:T(8,128)S(1)}, f32[18,30,256]{2,1,0:T(8,128)S(1)}, u32[]{:S(2)}, u32[]{:S(2)}) collective-permute-start(f32[18,30,256]{2,1,0:T(8,128)S(1)} %reshape.118), channel_id=1, source_target_pairs={{0,2},{2,4},{4,6},{6,8},{8,10},{10,12},{12,14},{14,16},{16,18},{18... | collective-permute-start | bytes 1658888 | tf_op jit(solution)/shard_map/ppermute | solution.py:28
  131.8 29.6 %collective-permute-start.11 = (f32[18,30,256]{2,1,0:T(8,128)S(1)}, f32[18,30,256]{2,1,0:T(8,128)S(1)}, u32[]{:S(2)}, u32[]{:S(2)}) collective-permute-start(f32[18,30,256]{2,1,0:T(8,128)S(1)} %reshape.119), channel_id=1, source_target_pairs={{2,0},{4,2},{6,4},{8,6},{10,8},{12,10},{14,12},{16,14},{18,16},{20... | collective-permute-start | bytes 1658888 | tf_op jit(solution)/shard_map/ppermute | solution.py:28
  166.3 2.3 %copy-start.10 = (bf16[1024,1024]{1,0:T(8,128)(2,1)S(1)}, bf16[1024,1024]{1,0:T(8,128)(2,1)}, u32[]{:S(2)}) copy-start(bf16[1024,1024]{1,0:T(8,128)(2,1)} %get-tuple-element.39) | copy-start | bytes 6291460
  166.3 2.3 %copy-start.30 = (f32[540]{0:T(1024)S(1)}, f32[540]{0:T(1024)}, u32[]{:S(2)}) copy-start(f32[540]{0:T(1024)} %mul.133) | copy-start | bytes 6484
  168.5 2.8 %copy-start.13 = (bf16[512,1024]{1,0:T(8,128)(2,1)S(1)}, bf16[512,1024]{1,0:T(8,128)(2,1)}, u32[]{:S(2)}) copy-start(bf16[512,1024]{1,0:T(8,128)(2,1)} %copy-done.11) | copy-start | bytes 3145732
  175.2 1.4 collective-permute-start.12
  175.8 1.3 collective-permute-start.13
  (16 other events, 17.7 us)

commit v2 on v1

v2 whole, which is shorter than its diff:
```python
import functools
import math

import jax
import jax.numpy as jnp
from jax import lax
from jax.experimental import pallas as pl
from jax.experimental.pallas import tpu as pltpu
from jax.sharding import PartitionSpec as P

NDIR = 36
ITERS = 3
CHUNKS = 2
FACE_TILE = 256
MESH = pl.DeviceIdType.MESH


def exchange_kernel(mine_ref, all_ref, send_sem, recv_sem):
    count = lax.axis_size("rows")
    me = lax.axis_index("rows")
    barrier = pltpu.get_barrier_semaphore()
    for hop in range(1, count):
        pl.semaphore_signal(
            barrier,
            inc=1,
            device_id={"rows": lax.rem(me + hop, count)},
            device_id_type=MESH,
        )
    pl.semaphore_wait(barrier, count - 1)

    def copy(hop):
        return pltpu.make_async_remote_copy(
            src_ref=mine_ref,
            dst_ref=all_ref.at[hop],
            send_sem=send_sem.at[hop],
            recv_sem=recv_sem.at[hop],
            device_id={"rows": lax.rem(me + hop, count)},
            device_id_type=MESH,
        )

    for hop in range(1, count):
        copy(hop).start()
    all_ref[0] = mine_ref[...]
    for hop in range(1, count):
        copy(hop).wait()


def exchange(block):
    count = lax.axis_size("rows")
    return pl.pallas_call(
        exchange_kernel,
        out_shape=jax.ShapeDtypeStruct((count,) + block.shape, block.dtype),
        in_specs=[pl.BlockSpec(memory_space=pltpu.VMEM)],
        out_specs=pl.BlockSpec(memory_space=pltpu.VMEM),
        scratch_shapes=[
            pltpu.SemaphoreType.DMA((count,)),
            pltpu.SemaphoreType.DMA((count,)),
        ],
        compiler_params=pltpu.CompilerParams(collective_id=0, has_side_effects=True),
    )(block)


def pieces(value):
    high = value.astype(jnp.bfloat16)
    low = (value - high.astype(jnp.float32)).astype(jnp.bfloat16)
    return high, low


def steps_kernel(
    nfreq,
    field_ref,
    lower_row_ref,
    upper_row_ref,
    lower_col_ref,
    upper_col_ref,
    slots_ref,
    cells_ref,
    forward_ref,
    backward_ref,
    gain_ref,
    area_ref,
    turn_ref,
    out_ref,
    current,
    lhs,
    moved,
    own_hot,
    up_hot,
    signed_hot,
    pick_hot,
    flux_sum,
    halo_out,
    halo_in,
    rim_out,
    rim_in,
    halo_send_sem,
    halo_recv_sem,
    rim_send_sem,
    rim_recv_sem,
):
    rows_n = lax.axis_size("rows")
    me = lax.axis_index("rows")
    spec_n = lax.axis_size("spec")
    shard = lax.axis_index("spec")
    prev = lax.rem(shard + spec_n - 1, spec_n)
    following = lax.rem(shard + 1, spec_n)
    _, dloc, fsize, cdev = current.shape
    fdev = own_hot.shape[1]
    rows = dloc * fsize
    width = halo_in.shape[3]
    has_above = me < rows_n - 1
    has_below = me > 0

    barrier = pltpu.get_barrier_semaphore()

    @pl.when(has_above)
    def _():
        pl.semaphore_signal(barrier, inc=1, device_id={"rows": me + 1}, device_id_type=MESH)

    @pl.when(has_below)
    def _():
        pl.semaphore_signal(barrier, inc=1, device_id={"rows": me - 1}, device_id_type=MESH)

    others = (prev,) if spec_n == 2 else (prev, following)
    for other in others:
        pl.semaphore_signal(barrier, inc=1, device_id={"spec": other}, device_id_type=MESH)

    cell_ids = lax.broadcasted_iota(jnp.int32, (cdev, 2 * width), 0)
    pick_hot[...] = jnp.where(cell_ids == cells_ref[...], 1.0, 0.0).astype(jnp.bfloat16)
    for chunk in range(CHUNKS):
        first = chunk * fsize
        here = min(fsize, nfreq - first)
        current[chunk, :, :here, :] = field_ref[:, first : first + here, :]
        if here < fsize:
            current[chunk, :, here:, :] = jnp.zeros((dloc, fsize - here, cdev), jnp.float32)

    row_peers = jnp.where(has_above, 1, 0) + jnp.where(has_below, 1, 0)
    pl.semaphore_wait(barrier, len(others) + row_peers)

    def to_above(turn):
        return pltpu.make_async_remote_copy(
            src_ref=halo_out.at[turn, 0],
            dst_ref=halo_in.at[turn, 0],
            send_sem=halo_send_sem.at[turn, 0],
            recv_sem=halo_recv_sem.at[turn, 0],
            device_id={"rows": me + 1},
            device_id_type=MESH,
        )

    def to_below(turn):
        return pltpu.make_async_remote_copy(
            src_ref=halo_out.at[turn, 1],
            dst_ref=halo_in.at[turn, 1],
            send_sem=halo_send_sem.at[turn, 1],
            recv_sem=halo_recv_sem.at[turn, 1],
            device_id={"rows": me - 1},
            device_id_type=MESH,
        )

    def rim_copy(turn, side):
        return pltpu.make_async_remote_copy(
            src_ref=rim_out.at[turn, side],
            dst_ref=rim_in.at[turn, side],
            send_sem=rim_send_sem.at[turn, side],
            recv_sem=rim_recv_sem.at[turn, side],
            device_id={"spec": following if side == 0 else prev},
            device_id_type=MESH,
        )

    def split_and_send(turn, chunk):
        value = current[chunk].reshape(rows, cdev)
        high, low = pieces(value)
        lhs[chunk, :rows] = high
        lhs[chunk, rows:] = low

        @pl.when(turn < CHUNKS * ITERS)
        def _():
            picked = jnp.dot(lhs[chunk], pick_hot[...], preferred_element_type=jnp.float32)
            total = picked[:rows] + picked[rows:]
            halo_out[turn, 0] = total[:, :width]
            halo_out[turn, 1] = total[:, width:]

            @pl.when(has_above)
            def _():
                to_above(turn).start()

            @pl.when(has_below)
            def _():
                to_below(turn).start()

    def first_send(chunk, carry):
        split_and_send(chunk, chunk)
        return carry

    lax.fori_loop(0, CHUNKS, first_send, 0)

    @pl.when(jnp.logical_not(has_below))
    def _():
        for turn in range(CHUNKS * ITERS):
            halo_in[turn, 0] = jnp.zeros((rows, width), jnp.float32)

    @pl.when(jnp.logical_not(has_above))
    def _():
        for turn in range(CHUNKS * ITERS):
            halo_in[turn, 1] = jnp.zeros((rows, width), jnp.float32)

    def one_hot(mask):
        return jnp.where(mask, 1.0, 0.0)

    for tile in range(fdev // FACE_TILE):
        faces = pl.ds(tile * FACE_TILE, FACE_TILE)
        ids = lax.broadcasted_iota(jnp.int32, (cdev, FACE_TILE), 0)
        own_hot[:, faces] = one_hot(ids == lower_row_ref[:, faces]).astype(jnp.bfloat16)
        up_hot[:cdev, faces] = one_hot(ids == upper_row_ref[:, faces]).astype(jnp.bfloat16)
        up_hot[cdev:, faces] = one_hot(slots_ref[...] == upper_row_ref[:, faces]).astype(
            jnp.bfloat16
        )
        lanes = lax.broadcasted_iota(jnp.int32, (FACE_TILE, cdev), 1)
        signed_hot[faces, :] = (
            one_hot(lanes == lower_col_ref[faces, :]) - one_hot(lanes == upper_col_ref[faces, :])
        ).astype(jnp.bfloat16)

    turn_rate = turn_ref[...]
    ahead = jnp.maximum(turn_rate, 0.0)
    back = jnp.minimum(turn_rate, 0.0)

    def one_turn(turn, carry):
        chunk = lax.rem(turn, CHUNKS)

        @pl.when(has_below)
        def _():
            to_above(turn).wait_recv()

        @pl.when(has_above)
        def _():
            to_below(turn).wait_recv()

        halos = []
        for side in range(2):
            high, low = pieces(halo_in[turn, side])
            halos.append(jnp.concatenate([high, low], axis=0))
        halo = jnp.concatenate(halos, axis=1)
        flux_sum[...] = jnp.zeros_like(flux_sum)

        def face_tile(tile, inner):
            faces = pl.ds(pl.multiple_of(tile * FACE_TILE, FACE_TILE), FACE_TILE)
            own = lhs[chunk]
            low_vals = jnp.dot(own, own_hot[:, faces], preferred_element_type=jnp.float32)
            up_vals = jnp.dot(own, up_hot[:cdev, faces], preferred_element_type=jnp.float32)
            up_vals += jnp.dot(halo, up_hot[cdev:, faces], preferred_element_type=jnp.float32)
            low_vals = (low_vals[:rows] + low_vals[rows:]).reshape(dloc, fsize, FACE_TILE)
            up_vals = (up_vals[:rows] + up_vals[rows:]).reshape(dloc, fsize, FACE_TILE)
            flux = forward_ref[:, :, faces] * low_vals + backward_ref[:, :, faces] * up_vals
            high, low = pieces(flux.reshape(rows, FACE_TILE))
            both = jnp.concatenate([high, low], axis=0)
            flux_sum[...] += jnp.dot(
                both, signed_hot[faces, :], preferred_element_type=jnp.float32
            )
            return inner

        lax.fori_loop(0, fdev // FACE_TILE, face_tile, 0)
        total = (flux_sum[:rows] + flux_sum[rows:]).reshape(dloc, fsize, cdev)
        scale = gain_ref[chunk] * area_ref[...]
        moved[...] = current[chunk] - total * scale[None]
        rim_out[turn, 0] = moved[dloc - 1]
        rim_out[turn, 1] = moved[0]
        rim_copy(turn, 0).start()
        rim_copy(turn, 1).start()
        mid = moved[1 : dloc - 1]
        current[chunk, 1 : dloc - 1] = (
            mid - ahead * (mid - moved[: dloc - 2]) - back * (moved[2:] - mid)
        )
        rim_copy(turn, 0).wait_recv()
        rim_copy(turn, 1).wait_recv()
        edge = moved[0]
        current[chunk, 0] = edge - ahead * (edge - rim_in[turn, 0]) - back * (moved[1] - edge)
        edge = moved[dloc - 1]
        current[chunk, dloc - 1] = (
            edge - ahead * (edge - moved[dloc - 2]) - back * (rim_in[turn, 1] - edge)
        )
        split_and_send(turn + CHUNKS, chunk)
        return carry

    lax.fori_loop(0, CHUNKS * ITERS, one_turn, 0)

    for chunk in range(CHUNKS):
        first = chunk * fsize
        here = min(fsize, nfreq - first)
        out_ref[:, first : first + here, :] = current[chunk, :, :here, :]

    def drain(turn, carry):
        rim_copy(turn, 0).wait_send()
        rim_copy(turn, 1).wait_send()

        @pl.when(has_above)
        def _():
            to_above(turn).wait_send()

        @pl.when(has_below)
        def _():
            to_below(turn).wait_send()

        return carry

    lax.fori_loop(0, CHUNKS * ITERS, drain, 0)


def run_steps(collective_id, width, slots, cells, field, faces, forward, backward, gain, area, turn):
    dloc, nfreq, cdev = field.shape
    fdev = faces.shape[1]
    fsize = gain.shape[1]
    rows = dloc * fsize
    turns = CHUNKS * ITERS
    vmem = pl.BlockSpec(memory_space=pltpu.VMEM)
    operands = (
        field,
        faces[0:1],
        faces[1:2],
        faces[0][:, None],
        faces[1][:, None],
        slots,
        cells,
        forward[:, None, :],
        backward[:, None, :],
        gain,
        area[None, :],
        turn[None, :],
    )
    return pl.pallas_call(
        functools.partial(steps_kernel, nfreq),
        out_shape=jax.ShapeDtypeStruct(field.shape, jnp.float32),
        in_specs=[vmem] * len(operands),
        out_specs=vmem,
        scratch_shapes=[
            pltpu.VMEM((CHUNKS, dloc, fsize, cdev), jnp.float32),
            pltpu.VMEM((CHUNKS, 2 * rows, cdev), jnp.bfloat16),
            pltpu.VMEM((dloc, fsize, cdev), jnp.float32),
            pltpu.VMEM((cdev, fdev), jnp.bfloat16),
            pltpu.VMEM((cdev + 2 * width, fdev), jnp.bfloat16),
            pltpu.VMEM((fdev, cdev), jnp.bfloat16),
            pltpu.VMEM((cdev, 2 * width), jnp.bfloat16),
            pltpu.VMEM((2 * rows, cdev), jnp.float32),
            pltpu.VMEM((turns, 2, rows, width), jnp.float32),
            pltpu.VMEM((turns, 2, rows, width), jnp.float32),
            pltpu.VMEM((turns, 2, fsize, cdev), jnp.float32),
            pltpu.VMEM((turns, 2, fsize, cdev), jnp.float32),
            pltpu.SemaphoreType.DMA((turns, 2)),
            pltpu.SemaphoreType.DMA((turns, 2)),
            pltpu.SemaphoreType.DMA((turns, 2)),
            pltpu.SemaphoreType.DMA((turns, 2)),
        ],
        compiler_params=pltpu.CompilerParams(
            collective_id=collective_id, has_side_effects=True, vmem_limit_bytes=60 * 2**20
        ),
    )(*operands)


def on_device(
    field,
    group_speed,
    face_angle,
    face_speed,
    face_cells,
    face_live,
    halo_blocks,
    cell_level,
    polar_mask,
    turn_rate,
):
    dloc, nfreq, cdev = field.shape
    fdev = face_angle.shape[0]
    rows_n = lax.axis_size("rows")
    me = lax.axis_index("rows")
    first_dir = lax.axis_index("spec") * dloc
    theta = ((first_dir + jnp.arange(dloc, dtype=jnp.int32)).astype(jnp.float32) + 0.5) * (
        2.0 * math.pi / NDIR
    )
    turn = polar_mask.astype(jnp.float32) * turn_rate
    area = jnp.exp2(-cell_level.astype(jnp.float32))
    live = jnp.arange(fdev, dtype=jnp.int32) < face_live[0] * 128
    slot_weight = face_speed * live.astype(jnp.float32)
    cosine = jnp.cos(theta[:, None] - face_angle[None, :]) * slot_weight[None, :]
    forward = jnp.maximum(cosine, 0.0)
    backward = jnp.minimum(cosine, 0.0)
    fsize = 8 * (-(-nfreq // (8 * CHUNKS)))
    gain = jnp.pad(group_speed, (0, CHUNKS * fsize - nfreq)).reshape(CHUNKS, fsize, 1)

    table = halo_blocks[0]
    full = 128 * table.shape[1]
    half = full // 2
    spots = jnp.arange(2 * full, dtype=jnp.int32)
    asked = jnp.any(
        (spots[:, None] + cdev == face_cells[1][None, :]) & live[None, :], axis=1
    ).reshape(2, full)
    spot = jnp.arange(full, dtype=jnp.int32)
    rank = jnp.sum(
        jnp.where(asked[:, None, :] & (spot[None, None, :] < spot[None, :, None]), 1, 0), axis=2
    )
    cells_full = (table[:, :, None] * 128 + jnp.arange(128, dtype=jnp.int32)).reshape(2, full)
    slots_full = cdev + spots.reshape(2, full)
    order = jnp.arange(half, dtype=jnp.int32)
    hit = asked[:, None, :] & (rank[:, None, :] == order[None, :, None])
    cells_half = jnp.sum(jnp.where(hit, cells_full[:, None, :] + 1, 0), axis=2) - 1
    slots_half = jnp.sum(jnp.where(hit, slots_full[:, None, :] + 1, 0), axis=2) - 1
    most = jnp.max(jnp.sum(asked.astype(jnp.int32), axis=1))
    width = max(full, 128)
    block = jnp.stack(
        [jnp.pad(cells_half[side], (0, width - half)) for side in range(2)]
        + [cells_full[0], cells_full[1], jnp.full((width,), most)]
    )
    block = jnp.pad(block, ((0, 8 - block.shape[0]), (0, 0)))
    lists = exchange(block)
    fits = jnp.max(lists[:, 4, 0]) <= half
    from_below = lists[1]
    from_above = lists[rows_n - 1]
    shared = (field, face_cells, forward, backward, gain, area, turn)

    def narrow(args):
        cells = jnp.concatenate([from_above[0, :half], from_below[1, :half]])[None, :]
        return run_steps(1, half, slots_half.reshape(-1, 1), cells, *args)

    def wide(args):
        cells = jnp.concatenate([from_above[2], from_below[3]])[None, :]
        return run_steps(2, full, slots_full.reshape(-1, 1), cells, *args)

    return lax.cond(fits, narrow, wide, shared)


def solution(mesh):
    return jax.shard_map(
        on_device,
        mesh=mesh,
        in_specs=(
            P("spec", None, "rows"),
            P(),
            P("rows"),
            P("rows"),
            P(None, "rows"),
            P("rows"),
            P("rows", None, None),
            P("rows"),
            P("rows"),
            P("rows"),
        ),
        out_specs=P("spec", None, "rows"),
        check_vma=False,
    )
```

time: 179 us -> 87.5 us (0.49)
  the two profiles are of different devices: /device:TPU:13 before, /device:TPU:0 now
where the time goes in v2:
time: 87.5 us; the launch traced here: 86.9 us
  Pallas kernels  67.5 us (77%)
  local copies, waits for them, and re-layouts  10.8 us (12%)
  other arithmetic  7.05 us (8%)
  between operations  1.44 us (2%)
    pallas_call x1, Pallas kernels, run_steps(): pl.pallas_call(functools.partial(steps_kernel, nfreq), out_shape=jax.Shap...  55.9 us
    pallas_call x1, Pallas kernels, exchange(): pl.pallas_call(exchange_kernel, out_shape=jax.ShapeDtypeStruct((count,) +...  11.6 us
    squeeze x2, local copies, waits for them, and re-layouts, run_steps(): faces[1][:, None]  2.39 us

profile of v2, /device:TPU:0, one launch (start us, length us, event | category | flops | bytes accessed | tf_op | source)
XLA Modules:
  0.0 86.9 jit_solution(14272610601019604147)
XLA Ops:
  0.7 0.7 pad.18
  1.3 0.1 reshape.98
  1.4 0.7 multiply_bitcast_fusion
  2.2 0.1 iota_add_fusion
  2.2 0.7 broadcast_select_fusion
  2.9 0.7 slice.60
  3.6 0.4 and_reduce_fusion
  4.1 0.1 convert_reduce_fusion
  4.2 0.6 reduce_max.18
  4.9 0.6 stack_broadcast_in_dim.3
  5.5 0.7 convert_multiply_fusion
  6.3 0.2 select_reduce_fusion.1
  6.4 0.1 select_reduce_fusion.2
  6.6 0.6 pad.17.mine_ref
  7.2 0.1 fusion
  7.3 11.6 %shard_map.102 = s32[16,8,256]{2,1,0:T(8,128)} custom-call(s32[8,256]{1,0:T(8,128)} %pad.17.mine_ref), custom_call_target="tpu_custom_call" | custom-call | tf_op jit(solution)/shard_map/pallas_call | solution.py:50
  18.9 1.5 %slice_reduce_fusion = s32[]{:T(128)} fusion(s32[16,8,256]{2,1,0:T(8,128)} %shard_map.102), kind=kLoop, calls=%fused_computation.23 | loop fusion | flops 15 | bytes 68 | tf_op jit(solution)/shard_map/reduce_max | solution.py:413
  21.0 0.7 slice_bitcast_fusion.6
  21.8 1.1 %fusion.1 = (f32[18,1024]{1,0:T(8,128)S(1)}, f32[18,1024]{1,0:T(8,128)S(1)}) fusion(f32[1024]{0:T(1024)S(1)} %broadcast_select_fusion, f32[1024]{0:T(1024)} %param.14, f32[18]{0:T(128)S(1)} %add_multiply_fusion), kind=kLoop, calls=%fused_computation.19 | loop fusion | flops 73728 | bytes 155720 | tf_op jit(solution)/shard_map/min | solution.py:384
  22.9 63.0 %conditional.1 = (f32[18,30,512]{2,1,0:T(8,128)S(1)}) conditional(s32[]{:T(128)} %convert_element_type.23, (s32[2,1024]{1,0:T(2,128)}, s32[2,256]{1,0:T(2,128)S(1)}, s32[2,256]{1,0:T(2,128)S(1)}, s32[8,256]{1,0:T(8,128)S(1)}, s32[8,256]{1,0:T(8,128)S(1)}, /*index=5*/f32[18,1024]{1,0:T(8,128)S(1)}, f32[18,1024]{1,0:T(8,128)S(1)}, f32[512]{0:T(512)S(1)}, ...), branch_computations={%region_6.7_spmd, %region_7.9_spmd} | conditional | flops 132864 | bytes 5110052 | solution.py:426
  22.9 0.0 copy-start.1
  22.9 0.6 pad_add_fusion.1
  23.5 0.1 select_reduce_fusion
  23.7 0.7 copy.30.gain_ref
  24.3 1.4 %slice_bitcast_fusion.4 = (s32[1024,1]{0,1:T(1,128)S(1)}, s32[1024,1]{0,1:T(1,128)S(1)}, s32[1,1024]{1,0:T(1,128)}, s32[1,1024]{1,0:T(1,128)}) fusion(s32[2,1024]{1,0:T(2,128)} %get-tuple-element.120), kind=kLoop, calls=%fused_computation.10 | loop fusion | bytes 24576 | tf_op jit(solution)/shard_map/cond/branch_1_fun/broadcast_in_dim;cond/branch_1_fun/squeeze | solution.py:320
  25.7 0.7 broadcast_in_dim.66.backward_ref
  26.4 0.7 broadcast_in_dim.65.forward_ref
  27.1 0.8 copy.28.slots_ref
  27.9 1.0 %copy.27.upper_col_ref = s32[1024,1]{1,0:T(8,128)} copy(s32[1024,1]{0,1:T(1,128)S(1)} %get-tuple-element.213) | data formatting | bytes 8192 | tf_op jit(solution)/shard_map/cond/branch_1_fun/broadcast_in_dim;cond/branch_1_fun/squeeze | solution.py:320
  28.9 1.0 %copy.26.lower_col_ref = s32[1024,1]{1,0:T(8,128)} copy(s32[1024,1]{0,1:T(1,128)S(1)} %get-tuple-element.214) | data formatting | bytes 8192 | tf_op jit(solution)/shard_map/cond/branch_1_fun/broadcast_in_dim;cond/branch_1_fun/squeeze | solution.py:319
  29.9 55.9 %branch_1_fun.2 = f32[18,30,512]{2,1,0:T(8,128)S(1)} custom-call(f32[18,30,512]{2,1,0:T(8,128)S(1)} %copy-done.1, s32[1,1024]{1,0:T(1,128)} %get-tuple-element.215.lower_row_ref, s32[1,1024]{1,0:T(1,128)} %get-tuple-element.216.upper_row_ref, s32[1024,1]{1,0:T(8,128)} %copy.26.lower_col_ref, s32[1024,1]{1,0:T(8,128)} %copy.27.upper_col_ref, ...), custom_call_target="tpu_custom_call" | custom-call | tf_op jit(solution)/shard_map/cond/branch_1_fun/pallas_call | solution.py:329
  85.9 1.0 %copy.42 = f32[18,30,512]{2,1,0:T(8,128)} copy(f32[18,30,512]{2,1,0:T(8,128)S(1)} %get-tuple-element.133) | data formatting | bytes 2211840
  (24 shorter events, 0.2 us)
Async XLA Ops:
  22.9 7.0 %copy-start.1 = (f32[18,30,512]{2,1,0:T(8,128)S(1)}, f32[18,30,512]{2,1,0:T(8,128)}, u32[]{:S(2)}) copy-start(f32[18,30,512]{2,1,0:T(8,128)} %get-tuple-element.119.field_ref) | copy-start | bytes 3317764 | tf_op jit(solution)/shard_map/cond

commit v3 on v2

v3 whole, which is shorter than its diff:
```python
import functools
import math

import jax
import jax.numpy as jnp
from jax import lax
from jax.experimental import pallas as pl
from jax.experimental.pallas import tpu as pltpu
from jax.sharding import PartitionSpec as P

NDIR = 36
ITERS = 3
CHUNKS = 2
FACE_TILE = 256
MESH = pl.DeviceIdType.MESH


def exchange_kernel(
    cdev,
    half,
    faces_ref,
    live_ref,
    table_ref,
    cells_ref,
    slots_ref,
    most_ref,
    above_ref,
    below_ref,
    mine,
    every,
    send_sem,
    recv_sem,
):
    count = lax.axis_size("rows")
    me = lax.axis_index("rows")
    barrier = pltpu.get_barrier_semaphore()
    for hop in range(1, count):
        pl.semaphore_signal(
            barrier,
            inc=1,
            device_id={"rows": lax.rem(me + hop, count)},
            device_id_type=MESH,
        )

    fdev = faces_ref.shape[1]
    blocks = table_ref.shape[2]
    full = 128 * blocks
    face = lax.broadcasted_iota(jnp.int32, (1, fdev), 1)
    upper = jnp.where(face < live_ref[0] * 128, faces_ref[1:2, :], -1)
    below_diagonal = lax.broadcasted_iota(jnp.int32, (full, full), 1) < lax.broadcasted_iota(
        jnp.int32, (full, full), 0
    )
    triangle = jnp.where(below_diagonal, 1.0, 0.0).astype(jnp.bfloat16)
    spot = lax.broadcasted_iota(jnp.int32, (full, half), 0)
    order = lax.broadcasted_iota(jnp.int32, (full, half), 1).astype(jnp.float32)
    mine[...] = jnp.zeros_like(mine)
    most = jnp.zeros((1, half), jnp.float32)
    for side in range(2):
        base = cdev + side * full
        spots = lax.broadcasted_iota(jnp.int32, (full, fdev), 0) + base
        asked = jnp.max(jnp.where(spots == upper, 1.0, 0.0), axis=1, keepdims=True)
        asked = jnp.broadcast_to(asked, (full, half))
        rank = jnp.dot(triangle, asked.astype(jnp.bfloat16), preferred_element_type=jnp.float32)
        hit = jnp.where(rank == order, asked, 0.0)
        cell = spot
        for k in range(blocks):
            inside = (spot >= 128 * k) & (spot < 128 * (k + 1))
            cell = jnp.where(inside, table_ref[0, side, k] * 128 + spot - 128 * k, cell)
            row = 3 + side * blocks + k
            mine[row : row + 1, :] = jnp.full((1, half), table_ref[0, side, k], jnp.int32)

        def listed(values):
            total = jnp.sum(hit * (values + 1).astype(jnp.float32), axis=0, keepdims=True)
            return total.astype(jnp.int32) - 1

        mine[side : side + 1, :] = listed(cell)
        slots_ref[:, side * half : (side + 1) * half] = listed(spot + base)
        most = jnp.maximum(most, jnp.sum(asked, axis=0, keepdims=True))
    mine[2:3, :] = most.astype(jnp.int32)

    pl.semaphore_wait(barrier, count - 1)

    def copy(hop):
        return pltpu.make_async_remote_copy(
            src_ref=mine,
            dst_ref=every.at[hop],
            send_sem=send_sem.at[hop],
            recv_sem=recv_sem.at[hop],
            device_id={"rows": lax.rem(me + hop, count)},
            device_id_type=MESH,
        )

    for hop in range(1, count):
        copy(hop).start()
    highest = mine[2:3, :]
    for hop in range(1, count):
        copy(hop).wait()
        highest = jnp.maximum(highest, every[hop, 2:3, :])
    most_ref[...] = highest
    above_ref[...] = every[count - 1]
    below_ref[...] = every[1]
    cells_ref[:, :half] = every[count - 1, 0:1, :]
    cells_ref[:, half:] = every[1, 1:2, :]


def exchange(cdev, half, faces, live, table):
    count = lax.axis_size("rows")
    vmem = pl.BlockSpec(memory_space=pltpu.VMEM)
    smem = pl.BlockSpec(memory_space=pltpu.SMEM)
    height = 8 * (-(-(3 + 2 * table.shape[2]) // 8))
    shapes = ((1, 2 * half), (1, 2 * half), (1, half), (height, half), (height, half))
    return pl.pallas_call(
        functools.partial(exchange_kernel, cdev, half),
        out_shape=[jax.ShapeDtypeStruct(shape, jnp.int32) for shape in shapes],
        in_specs=[vmem, smem, smem],
        out_specs=[vmem] * len(shapes),
        scratch_shapes=[
            pltpu.VMEM((height, half), jnp.int32),
            pltpu.VMEM((count, height, half), jnp.int32),
            pltpu.SemaphoreType.DMA((count,)),
            pltpu.SemaphoreType.DMA((count,)),
        ],
        compiler_params=pltpu.CompilerParams(collective_id=0, has_side_effects=True),
    )(faces, live, table)


def pieces(value):
    high = value.astype(jnp.bfloat16)
    low = (value - high.astype(jnp.float32)).astype(jnp.bfloat16)
    return high, low


def steps_kernel(
    nfreq,
    field_ref,
    faces_ref,
    slots_ref,
    cells_ref,
    cosine_ref,
    group_speed_ref,
    level_ref,
    mask_ref,
    rate_ref,
    out_ref,
    forward_ref,
    backward_ref,
    scale_ref,
    current,
    lhs,
    moved,
    own_hot,
    up_hot,
    signed_hot,
    pick_hot,
    flux_sum,
    halo_out,
    halo_in,
    rim_out,
    rim_in,
    halo_send_sem,
    halo_recv_sem,
    rim_send_sem,
    rim_recv_sem,
):
    rows_n = lax.axis_size("rows")
    me = lax.axis_index("rows")
    spec_n = lax.axis_size("spec")
    shard = lax.axis_index("spec")
    prev = lax.rem(shard + spec_n - 1, spec_n)
    following = lax.rem(shard + 1, spec_n)
    _, dloc, fsize, cdev = current.shape
    fdev = own_hot.shape[1]
    rows = dloc * fsize
    width = halo_in.shape[4]
    has_above = me < rows_n - 1
    has_below = me > 0

    barrier = pltpu.get_barrier_semaphore()

    @pl.when(has_above)
    def _():
        pl.semaphore_signal(barrier, inc=1, device_id={"rows": me + 1}, device_id_type=MESH)

    @pl.when(has_below)
    def _():
        pl.semaphore_signal(barrier, inc=1, device_id={"rows": me - 1}, device_id_type=MESH)

    others = (prev,) if spec_n == 2 else (prev, following)
    for other in others:
        pl.semaphore_signal(barrier, inc=1, device_id={"spec": other}, device_id_type=MESH)

    cell_ids = lax.broadcasted_iota(jnp.int32, (cdev, 2 * width), 0)
    pick_hot[...] = jnp.where(cell_ids == cells_ref[...], 1.0, 0.0).astype(jnp.bfloat16)
    for chunk in range(CHUNKS):
        first = chunk * fsize
        here = min(fsize, nfreq - first)
        current[chunk, :, :here, :] = field_ref[:, first : first + here, :]
        if here < fsize:
            current[chunk, :, here:, :] = jnp.zeros((dloc, fsize - here, cdev), jnp.float32)

    def kept(chunk):
        return pl.ds(0, fsize)

    def to_above(turn, chunk):
        return pltpu.make_async_remote_copy(
            src_ref=halo_out.at[turn, 0, :, kept(chunk), :],
            dst_ref=halo_in.at[turn, 0, :, kept(chunk), :],
            send_sem=halo_send_sem.at[turn, 0],
            recv_sem=halo_recv_sem.at[turn, 0],
            device_id={"rows": me + 1},
            device_id_type=MESH,
        )

    def to_below(turn, chunk):
        return pltpu.make_async_remote_copy(
            src_ref=halo_out.at[turn, 1, :, kept(chunk), :],
            dst_ref=halo_in.at[turn, 1, :, kept(chunk), :],
            send_sem=halo_send_sem.at[turn, 1],
            recv_sem=halo_recv_sem.at[turn, 1],
            device_id={"rows": me - 1},
            device_id_type=MESH,
        )

    def rim_copy(turn, side):
        return pltpu.make_async_remote_copy(
            src_ref=rim_out.at[turn, side],
            dst_ref=rim_in.at[turn, side],
            send_sem=rim_send_sem.at[turn, side],
            recv_sem=rim_recv_sem.at[turn, side],
            device_id={"spec": following if side == 0 else prev},
            device_id_type=MESH,
        )

    def split(chunk):
        high, low = pieces(current[chunk].reshape(rows, cdev))
        lhs[chunk, :rows] = high
        lhs[chunk, rows:] = low

    def pick(turn, chunk):
        picked = jnp.dot(lhs[chunk], pick_hot[...], preferred_element_type=jnp.float32)
        total = (picked[:rows] + picked[rows:]).reshape(dloc, fsize, 2 * width)
        halo_out[turn, 0] = total[:, :, :width]
        halo_out[turn, 1] = total[:, :, width:]

    def send(turn, chunk):
        @pl.when(has_above)
        def _():
            to_above(turn, chunk).start()

        @pl.when(has_below)
        def _():
            to_below(turn, chunk).start()

    for chunk in range(CHUNKS):
        split(chunk)
        pick(chunk, chunk)
        if chunk == 0:
            row_peers = jnp.where(has_above, 1, 0) + jnp.where(has_below, 1, 0)
            pl.semaphore_wait(barrier, len(others) + row_peers)
        send(chunk, chunk)

    @pl.when(jnp.logical_not(has_below))
    def _():
        for turn in range(CHUNKS * ITERS):
            halo_in[turn, 0] = jnp.zeros((dloc, fsize, width), jnp.float32)

    @pl.when(jnp.logical_not(has_above))
    def _():
        for turn in range(CHUNKS * ITERS):
            halo_in[turn, 1] = jnp.zeros((dloc, fsize, width), jnp.float32)

    def one_hot(mask):
        return jnp.where(mask, 1.0, 0.0)

    def as_column(row):
        return jnp.transpose(jnp.broadcast_to(row, (128, row.shape[1])))

    slot_column = as_column(slots_ref[...])
    for lane in range(fdev // 128):
        faces = pl.ds(lane * 128, 128)
        ids = lax.broadcasted_iota(jnp.int32, (cdev, 128), 0)
        lower = faces_ref[0:1, faces]
        upper = faces_ref[1:2, faces]
        own_hot[:, faces] = one_hot(ids == lower).astype(jnp.bfloat16)
        up_hot[:cdev, faces] = one_hot(ids == upper).astype(jnp.bfloat16)
        up_hot[cdev:, faces] = one_hot(slot_column == upper).astype(jnp.bfloat16)
        lower = as_column(lower)
        upper = as_column(upper)
        for part in range(cdev // 128):
            lanes = lax.broadcasted_iota(jnp.int32, (128, 128), 1) + part * 128
            signed_hot[faces, part * 128 : (part + 1) * 128] = (
                one_hot(lanes == lower) - one_hot(lanes == upper)
            ).astype(jnp.bfloat16)
    for d in range(dloc):
        forward_ref[d] = jnp.maximum(cosine_ref[d : d + 1, :], 0.0)
        backward_ref[d] = jnp.minimum(cosine_ref[d : d + 1, :], 0.0)
    area = 1.0 / lax.shift_left(jnp.ones_like(level_ref[...]), level_ref[...]).astype(jnp.float32)
    scale_ref[...] = jnp.zeros_like(scale_ref)
    for f in range(nfreq):
        at = f % fsize
        scale_ref[f // fsize, at : at + 1, :] = group_speed_ref[f] * area

    turn_rate = mask_ref[...].astype(jnp.float32) * rate_ref[...]
    ahead = jnp.maximum(turn_rate, 0.0)
    back = jnp.minimum(turn_rate, 0.0)

    def one_turn(step, chunk):
        turn = step * CHUNKS + chunk

        @pl.when(has_below)
        def _():
            to_above(turn, chunk).wait_recv()

        @pl.when(has_above)
        def _():
            to_below(turn, chunk).wait_recv()

        halos = []
        for side in range(2):
            high, low = pieces(halo_in[turn, side].reshape(rows, width))
            halos.append(jnp.concatenate([high, low], axis=0))
        halo = jnp.concatenate(halos, axis=1)
        flux_sum[...] = jnp.zeros_like(flux_sum)

        def face_tile(tile, inner):
            faces = pl.ds(pl.multiple_of(tile * FACE_TILE, FACE_TILE), FACE_TILE)
            own = lhs[chunk]
            low_vals = jnp.dot(own, own_hot[:, faces], preferred_element_type=jnp.float32)
            up_vals = jnp.dot(own, up_hot[:cdev, faces], preferred_element_type=jnp.float32)
            up_vals += jnp.dot(halo, up_hot[cdev:, faces], preferred_element_type=jnp.float32)
            low_vals = (low_vals[:rows] + low_vals[rows:]).reshape(dloc, fsize, FACE_TILE)
            up_vals = (up_vals[:rows] + up_vals[rows:]).reshape(dloc, fsize, FACE_TILE)
            flux = forward_ref[:, :, faces] * low_vals + backward_ref[:, :, faces] * up_vals
            high, low = pieces(flux.reshape(rows, FACE_TILE))
            both = jnp.concatenate([high, low], axis=0)
            flux_sum[...] += jnp.dot(
                both, signed_hot[faces, :], preferred_element_type=jnp.float32
            )
            return inner

        lax.fori_loop(0, fdev // FACE_TILE, face_tile, 0)
        total = (flux_sum[:rows] + flux_sum[rows:]).reshape(dloc, fsize, cdev)
        moved[...] = current[chunk] - total * scale_ref[chunk]
        rim_out[turn, 0] = moved[dloc - 1]
        rim_out[turn, 1] = moved[0]
        rim_copy(turn, 0).start()
        rim_copy(turn, 1).start()
        mid = moved[1 : dloc - 1]
        current[chunk, 1 : dloc - 1] = (
            mid - ahead * (mid - moved[: dloc - 2]) - back * (moved[2:] - mid)
        )
        rim_copy(turn, 0).wait_recv()
        rim_copy(turn, 1).wait_recv()
        edge = moved[0]
        current[chunk, 0] = edge - ahead * (edge - rim_in[turn, 0]) - back * (moved[1] - edge)
        edge = moved[dloc - 1]
        current[chunk, dloc - 1] = (
            edge - ahead * (edge - moved[dloc - 2]) - back * (rim_in[turn, 1] - edge)
        )

        @pl.when(step < ITERS - 1)
        def _():
            split(chunk)
            pick(turn + CHUNKS, chunk)
            send(turn + CHUNKS, chunk)

    def one_step(step, carry):
        for chunk in range(CHUNKS):
            one_turn(step, chunk)
        return carry

    lax.fori_loop(0, ITERS, one_step, 0)

    for chunk in range(CHUNKS):
        first = chunk * fsize
        here = min(fsize, nfreq - first)
        out_ref[:, first : first + here, :] = current[chunk, :, :here, :]

    def drain(step, carry):
        for chunk in range(CHUNKS):
            turn = step * CHUNKS + chunk
            rim_copy(turn, 0).wait_send()
            rim_copy(turn, 1).wait_send()

            @pl.when(has_above)
            def _(turn=turn, chunk=chunk):
                to_above(turn, chunk).wait_send()

            @pl.when(has_below)
            def _(turn=turn, chunk=chunk):
                to_below(turn, chunk).wait_send()

        return carry

    lax.fori_loop(0, ITERS, drain, 0)


def run_steps(collective_id, width, slots, cells, *rest):
    field, faces, cosine, group_speed, level, mask, rate = rest
    dloc, nfreq, cdev = field.shape
    fdev = faces.shape[1]
    fsize = 8 * (-(-nfreq // (8 * CHUNKS)))
    rows = dloc * fsize
    turns = CHUNKS * ITERS
    vmem = pl.BlockSpec(memory_space=pltpu.VMEM)
    smem = pl.BlockSpec(memory_space=pltpu.SMEM)
    operands = (field, faces, slots, cells, cosine, group_speed, level, mask, rate)
    return pl.pallas_call(
        functools.partial(steps_kernel, nfreq),
        out_shape=jax.ShapeDtypeStruct(field.shape, jnp.float32),
        in_specs=[vmem] * 5 + [smem] + [vmem] * 3,
        out_specs=vmem,
        scratch_shapes=[
            pltpu.VMEM((dloc, 1, fdev), jnp.float32),
            pltpu.VMEM((dloc, 1, fdev), jnp.float32),
            pltpu.VMEM((CHUNKS, fsize, cdev), jnp.float32),
            pltpu.VMEM((CHUNKS, dloc, fsize, cdev), jnp.float32),
            pltpu.VMEM((CHUNKS, 2 * rows, cdev), jnp.bfloat16),
            pltpu.VMEM((dloc, fsize, cdev), jnp.float32),
            pltpu.VMEM((cdev, fdev), jnp.bfloat16),
            pltpu.VMEM((cdev + 2 * width, fdev), jnp.bfloat16),
            pltpu.VMEM((fdev, cdev), jnp.bfloat16),
            pltpu.VMEM((cdev, 2 * width), jnp.bfloat16),
            pltpu.VMEM((2 * rows, cdev), jnp.float32),
            pltpu.VMEM((turns, 2, dloc, fsize, width), jnp.float32),
            pltpu.VMEM((turns, 2, dloc, fsize, width), jnp.float32),
            pltpu.VMEM((turns, 2, fsize, cdev), jnp.float32),
            pltpu.VMEM((turns, 2, fsize, cdev), jnp.float32),
            pltpu.SemaphoreType.DMA((turns, 2)),
            pltpu.SemaphoreType.DMA((turns, 2)),
            pltpu.SemaphoreType.DMA((turns, 2)),
            pltpu.SemaphoreType.DMA((turns, 2)),
        ],
        compiler_params=pltpu.CompilerParams(
            collective_id=collective_id, has_side_effects=True, vmem_limit_bytes=60 * 2**20
        ),
    )(*operands)


def on_device(
    field,
    group_speed,
    face_angle,
    face_speed,
    face_cells,
    face_live,
    halo_blocks,
    cell_level,
    polar_mask,
    turn_rate,
):
    dloc, nfreq, cdev = field.shape
    fdev = face_angle.shape[0]
    first_dir = lax.axis_index("spec") * dloc
    theta = ((first_dir + jnp.arange(dloc, dtype=jnp.int32)).astype(jnp.float32) + 0.5) * (
        2.0 * math.pi / NDIR
    )
    live = jnp.arange(fdev, dtype=jnp.int32) < face_live[0] * 128
    slot_weight = face_speed * live.astype(jnp.float32)
    cosine = jnp.cos(theta[:, None] - face_angle[None, :]) * slot_weight[None, :]
    blocks = halo_blocks.shape[2]
    full = 128 * blocks
    half = full // 2
    cells, slots, most, above, below = exchange(cdev, half, face_cells, face_live, halo_blocks)
    fits = most[0, 0] <= half
    shared = (
        field,
        face_cells,
        cosine,
        group_speed,
        cell_level[None, :],
        polar_mask[None, :],
        turn_rate[None, :],
    )

    def narrow(args):
        return run_steps(1, half, slots, cells, *args)

    def wide(args):
        tables = jnp.concatenate([above[3 : 3 + blocks, 0], below[3 + blocks : 3 + 2 * blocks, 0]])
        every_cell = tables[:, None] * 128 + jnp.arange(128, dtype=jnp.int32)
        every_slot = cdev + jnp.arange(2 * full, dtype=jnp.int32)
        return run_steps(2, full, every_slot[None, :], every_cell.reshape(1, -1), *args)

    return lax.cond(fits, narrow, wide, shared)


def solution(mesh):
    return jax.shard_map(
        on_device,
        mesh=mesh,
        in_specs=(
            P("spec", None, "rows"),
            P(),
            P("rows"),
            P("rows"),
            P(None, "rows"),
            P("rows"),
            P("rows", None, None),
            P("rows"),
            P("rows"),
            P("rows"),
        ),
        out_specs=P("spec", None, "rows"),
        check_vma=False,
    )
```

time: 87.5 us -> 70.7 us (0.81)
  local copies, waits for them, and re-layouts: 10.8 us -> 1.02 us
  other arithmetic: 7.05 us -> 1.79 us
  Pallas kernels: 67.5 us -> 66 us
    squeeze x6 -> x0, local copies, waits for them, and re-layouts: 4.15 us -> none  [the longest x2 2.39 us: run_steps(): faces[1][:, None]]
    reduce_max x2 -> x0, other arithmetic: 2.14 us -> none  [the longest x1 1.5 us: on_device(): fits = jnp.max(lists[:, 4, 0]) <= half]
    broadcast_in_dim x3 -> x0, local copies, waits for them, and re-layouts: 1.37 us -> none  [the longest x1 0.68 us: run_steps(): backward[:, None, :]]
    another operation x4 -> x0, local copies, waits for them, and re-layouts: 1.36 us -> none
    pad x4 -> x0, local copies, waits for them, and re-layouts: 1.27 us -> none  [the longest x1 0.66 us: on_device(): jnp.pad(group_speed, (0, CHUNKS * fsize - nfreq)).reshape(CHUNKS, fsize, 1)]
    pallas_call x1, Pallas kernels: 55.9 us -> 54.8 us  [run_steps(): pl.pallas_call(functools.partial(steps_kernel, nfreq), out_shape=jax.Shap...]
    min x1 -> x0, other arithmetic: 1.09 us -> none  [on_device(): backward = jnp.minimum(cosine, 0.0)]
    reshape x2 -> x0, local copies, waits for them, and re-layouts: 0.88 us -> none  [the longest x1 0.8 us: narrow(): return run_steps(1, half, slots_half.reshape(-1, 1), cells, *args)]
where the time goes in v3:
time: 70.7 us; the launch traced here: 70.3 us
  Pallas kernels  66 us (93%)
  other arithmetic  1.79 us (3%)
  between operations  1.3 us (2%)
  local copies, waits for them, and re-layouts  1.02 us (1%)
    pallas_call x1, Pallas kernels, run_steps(): pl.pallas_call(functools.partial(steps_kernel, nfreq), out_shape=jax.Shap...  54.8 us
    pallas_call x1, Pallas kernels, exchange(): pl.pallas_call(functools.partial(exchange_kernel, cdev, half), out_shape=...  11.2 us

profile of v3, /device:TPU:0, one launch (start us, length us, event | category | flops | bytes accessed | tf_op | source)
XLA Modules:
  0.0 70.3 jit_solution(8150418986112487826)
XLA Ops:
  0.7 0.7 fusion
  1.4 11.2 %shard_map.102 = (s32[1,256]{1,0:T(1,128)S(1)}, s32[1,256]{1,0:T(1,128)S(1)}, s32[1,128]{1,0:T(1,128)}, s32[8,128]{1,0:T(8,128)S(1)}, s32[8,128]{1,0:T(8,128)S(1)}) custom-call(s32[2,1024]{1,0:T(2,128)} %faces_ref.1, s32[1]{0:T(128)S(6)} %copy.18.live_ref, s32[1,2,2]{2,1,0:T(2,128)} %table_ref.1), custom_call_target="tpu_custom_call" | custom-call | tf_op jit(solution)/shard_map/pallas_call | solution.py:112
  13.2 1.1 %cosine_multiply_fusion = f32[18,1024]{1,0:T(8,128)S(1)} fusion(f32[1024]{0:T(1024)S(1)} %fusion, f32[1024]{0:T(1024)} %param.14, f32[18]{0:T(128)S(1)} %add_multiply_fusion.1), kind=kLoop, calls=%fused_computation.5 | loop fusion | flops 36864 | bytes 81992 | tf_op jit(solution)/shard_map/mul | solution.py:460
  14.3 55.0 %conditional.1 = (f32[18,30,512]{2,1,0:T(8,128)S(1)}) conditional(s32[]{:T(128)} %bitcast.3, (s32[8,128]{1,0:T(8,128)S(1)}, s32[8,128]{1,0:T(8,128)S(1)}, f32[18,30,512]{2,1,0:T(8,128)}, s32[2,1024]{1,0:T(2,128)}, f32[18,1024]{1,0:T(8,128)S(1)}, /*index=5*/f32[30]{0:T(128)}, s32[1,512]{1,0:T(1,128)}, s32[1,512]{1,0:T(1,128)}, ...), branch_computations={%region_0.0_spmd, %region_1.0_spmd} | conditional | flops 1032 | bytes 20568 | solution.py:485
  14.3 54.8 %branch_1_fun.1 = f32[18,30,512]{2,1,0:T(8,128)S(1)} custom-call(f32[18,30,512]{2,1,0:T(8,128)} %get-tuple-element.53.field_ref, s32[2,1024]{1,0:T(2,128)} %get-tuple-element.54.faces_ref, s32[1,256]{1,0:T(1,128)S(1)} %get-tuple-element.55.slots_ref, s32[1,256]{1,0:T(1,128)S(1)} %get-tuple-element.56.cells_ref, f32[18,1024]{1,0:T(8,128)S(1)} %get-tuple-element.57.cosine_ref, ...), custom_call_target="tpu_custom_call" | custom-call | tf_op jit(solution)/shard_map/cond/branch_1_fun/pallas_call | solution.py:408
  69.3 1.0 %copy.19 = f32[18,30,512]{2,1,0:T(8,128)} copy(f32[18,30,512]{2,1,0:T(8,128)S(1)} %get-tuple-element.72) | data formatting | bytes 2211840
  (1 shorter events, 0.0 us)

commit v4 on v3

--- a/solution.py
+++ b/solution.py
@@ -11,7 +11,7 @@
 NDIR = 36
 ITERS = 3
 CHUNKS = 2
-FACE_TILE = 256
+FACE_TILE = 512
 MESH = pl.DeviceIdType.MESH
 
 

time: 70.7 us -> 66.5 us (0.941)
  Pallas kernels: 66 us -> 61.8 us
    pallas_call x1, Pallas kernels: 54.8 us -> 50.6 us  [run_steps(): pl.pallas_call(functools.partial(steps_kernel, nfreq), out_shape=jax.Shap...]
where the time goes in v4:
time: 66.5 us; the launch traced here: 66.1 us
  Pallas kernels  61.8 us (93%)
  other arithmetic  1.79 us (3%)
  between operations  1.3 us (2%)
  local copies, waits for them, and re-layouts  1.02 us (2%)
    pallas_call x1, Pallas kernels, run_steps(): pl.pallas_call(functools.partial(steps_kernel, nfreq), out_shape=jax.Shap...  50.6 us
    pallas_call x1, Pallas kernels, exchange(): pl.pallas_call(functools.partial(exchange_kernel, cdev, half), out_shape=...  11.2 us

profile of v4, /device:TPU:0, one launch (start us, length us, event | category | flops | bytes accessed | tf_op | source)
XLA Modules:
  0.0 66.1 jit_solution(5125610674243476184)
XLA Ops:
  0.7 0.7 %fusion = f32[1024]{0:T(1024)S(1)} fusion(f32[1024]{0:T(1024)} %param.15, s32[]{:T(128)} %bitcast.4), kind=kLoop, calls=%fused_computation.7 | loop fusion | flops 2048 | bytes 8196 | tf_op jit(solution)/shard_map/mul | solution.py:459
  1.4 11.2 %shard_map.102 = (s32[1,256]{1,0:T(1,128)S(1)}, s32[1,256]{1,0:T(1,128)S(1)}, s32[1,128]{1,0:T(1,128)}, s32[8,128]{1,0:T(8,128)S(1)}, s32[8,128]{1,0:T(8,128)S(1)}) custom-call(s32[2,1024]{1,0:T(2,128)} %faces_ref.1, s32[1]{0:T(128)S(6)} %copy.18.live_ref, s32[1,2,2]{2,1,0:T(2,128)} %table_ref.1), custom_call_target="tpu_custom_call" | custom-call | tf_op jit(solution)/shard_map/pallas_call | solution.py:112
  13.2 1.1 %cosine_multiply_fusion = f32[18,1024]{1,0:T(8,128)S(1)} fusion(f32[1024]{0:T(1024)S(1)} %fusion, f32[1024]{0:T(1024)} %param.14, f32[18]{0:T(128)S(1)} %add_multiply_fusion.1), kind=kLoop, calls=%fused_computation.5 | loop fusion | flops 36864 | bytes 81992 | tf_op jit(solution)/shard_map/mul | solution.py:460
  14.3 50.8 %conditional.1 = (f32[18,30,512]{2,1,0:T(8,128)S(1)}) conditional(s32[]{:T(128)} %bitcast.3, (s32[8,128]{1,0:T(8,128)S(1)}, s32[8,128]{1,0:T(8,128)S(1)}, f32[18,30,512]{2,1,0:T(8,128)}, s32[2,1024]{1,0:T(2,128)}, f32[18,1024]{1,0:T(8,128)S(1)}, /*index=5*/f32[30]{0:T(128)}, s32[1,512]{1,0:T(1,128)}, s32[1,512]{1,0:T(1,128)}, ...), branch_computations={%region_0.0_spmd, %region_1.0_spmd} | conditional | flops 1032 | bytes 20568 | solution.py:485
  14.3 50.6 %branch_1_fun.1 = f32[18,30,512]{2,1,0:T(8,128)S(1)} custom-call(f32[18,30,512]{2,1,0:T(8,128)} %get-tuple-element.53.field_ref, s32[2,1024]{1,0:T(2,128)} %get-tuple-element.54.faces_ref, s32[1,256]{1,0:T(1,128)S(1)} %get-tuple-element.55.slots_ref, s32[1,256]{1,0:T(1,128)S(1)} %get-tuple-element.56.cells_ref, f32[18,1024]{1,0:T(8,128)S(1)} %get-tuple-element.57.cosine_ref, ...), custom_call_target="tpu_custom_call" | custom-call | tf_op jit(solution)/shard_map/cond/branch_1_fun/pallas_call | solution.py:408
  65.1 1.0 %copy.19 = f32[18,30,512]{2,1,0:T(8,128)} copy(f32[18,30,512]{2,1,0:T(8,128)S(1)} %get-tuple-element.72) | data formatting | bytes 2211840
  (1 shorter events, 0.0 us)
